TPU v7x, 256 devices: a 2x2x32 block of a 4x8x32 slice. The times are simulated.
256 devices in a mesh: groups: 4 (over x, y), blk: 64 (over z, core).
Axes of the slice: x: 2, y: 2, z: 32, core: 2. Of those that a mesh axis runs over, the one named last changes fastest.
The devices are a block of a 4x8x32 slice.
Arguments:
- snapshots: bfloat16 [4, 65536, 2, 64], P('groups', 'blk'), parts along dimension 0, may hold values from -6 to 6
- bin_index: int32 [4], P('groups'), parts along dimension 0, may hold values from 1 to 4095
- positions: int32 [3, 65536], replicated, may hold values from 0 to 511
- directions: int32 [3, 4096], replicated, may hold values from -128 to 127
- taper: float32 [65536], replicated, may hold values from 0.5 to 2
- beam_order: int32 [4096], replicated, may hold values from 0 to 4095, each once
Outputs:
- beams: bfloat16 [4096, 4, 2, 64], P('blk', 'groups'), parts along dimension 1
There are 4 independent parts, one for each index of `groups`. A program takes and returns all parts, laid end to end along the dimension named above; an argument that names none is the same for every part. Nothing has to cross between parts.
Inputs may be any that keep to these rules, and one draw needn't show every extreme that they name: beam_order is a permutation of the 4096 beams.
All inputs are finite; a program needn't handle non-finite values.
Results may differ from a plain program's by a relative error of at most 0.0048.
Values may be sent and summed in bfloat16 or wider, within the bound.
No kernel may reach another device: no remote copies, remote signals or barrier semaphores. Data moves between devices by JAX's collectives and lax.ppermute only.
A program may use at most 64 MiB of HBM per device.

v0:
```python
import math

import jax
import jax.numpy as jnp
from jax import lax
from jax.sharding import Mesh
from jax.sharding import PartitionSpec as P

ELEM = 65536
CYCLE = 8192
BLK = ("blk_0", "blk_1")


def sum_in_order(pieces, axes, sequence):
    lengths = [lax.axis_size(a) for a in axes]
    pieces = pieces.reshape(*lengths, *pieces.shape[1:])
    pieces = pieces.transpose(*sequence, *range(len(axes), pieces.ndim))
    pieces = pieces.reshape(-1, *pieces.shape[len(axes) :])
    for k in sequence:
        pieces = lax.psum_scatter(pieces, axes[k], scatter_dimension=0, tiled=True)
    return pieces[0]


def cut_along(value, dim, count):
    before, after = (value.shape[:dim], value.shape[dim + 1 :])
    return jnp.moveaxis(value.reshape(*before, count, -1, *after), dim, 0)


def scatter_axes(value, axes, sequence, dim):
    count = lax.axis_size(axes)
    return sum_in_order(cut_along(value, dim, count), axes, sequence)


def weight_block(dir_cols, positions, taper, bin_value):
    delays = dir_cols[0][:, None] * positions[0][None, :]
    delays = delays + dir_cols[1][:, None] * positions[1][None, :]
    delays = delays + dir_cols[2][:, None] * positions[2][None, :]
    delays = jnp.remainder(delays, CYCLE)
    phases = jnp.remainder(bin_value * delays, CYCLE)
    angles = phases.astype(jnp.float32) * (2.0 * math.pi / CYCLE)
    amplitude = taper / math.sqrt(ELEM)
    weight_re = (amplitude[None, :] * jnp.cos(angles)).astype(jnp.bfloat16)
    weight_im = (-amplitude[None, :] * jnp.sin(angles)).astype(jnp.bfloat16)
    return (weight_re, weight_im)


def beam_terms(dir_cols, positions, taper, snaps, bin_index):
    weight_re, weight_im = weight_block(dir_cols, positions, taper, bin_index[0])
    width = snaps.shape[3]
    columns = snaps[0].reshape(snaps.shape[1], 2 * width)
    with_real = jnp.dot(weight_re, columns, preferred_element_type=jnp.float32)
    with_imag = jnp.dot(weight_im, columns, preferred_element_type=jnp.float32)
    real_part = with_real[:, :width] - with_imag[:, width:]
    imag_part = with_real[:, width:] + with_imag[:, :width]
    results = [jnp.stack([real_part, imag_part], axis=1)]
    return jnp.stack(results, axis=1)


def blocked_terms(dir_cols, positions, taper, snaps, bin_index, row_block):
    count = dir_cols.shape[1]
    block_count = count // row_block
    blocks = dir_cols.reshape(3, block_count, row_block).transpose(1, 0, 2)

    def per_block(block_cols):
        return beam_terms(block_cols, positions, taper, snaps, bin_index)

    result = lax.map(per_block, blocks)
    return result.reshape(count, snaps.shape[0], 2, snaps.shape[3])


def per_device(snapshots, bin_index, positions, directions, taper, beam_order):
    ordered = jnp.take(directions, beam_order, axis=1)
    local_count = snapshots.shape[1]
    index = lax.axis_index(BLK)
    offset = index * local_count
    local_positions = lax.dynamic_slice_in_dim(positions, offset, local_count, 1)
    local_taper = lax.dynamic_slice_in_dim(taper, offset, local_count, 0)
    owned_rows = ordered.shape[1] // lax.axis_size(BLK)
    row_block = math.gcd(owned_rows * lax.axis_size(BLK), 512)
    summed = scatter_axes(
        blocked_terms(ordered, local_positions, local_taper, snapshots, bin_index, row_block),
        BLK,
        (1, 0),
        0,
    )
    return summed.astype(jnp.bfloat16)


def solution(mesh):
    split = Mesh(mesh.devices.reshape(mesh.shape["groups"], 32, 2), ("groups", "blk_0", "blk_1"))
    in_specs = (P("groups", BLK, None, None), P("groups"), P(), P(), P(), P())
    out_specs = P(BLK, "groups", None, None)
    return jax.shard_map(
        per_device, mesh=split, in_specs=in_specs, out_specs=out_specs, check_vma=False
    )
```

profile of v0, /device:TPU:38, one launch (start us, length us, event | category | flops | bytes accessed | tf_op | source)
XLA Modules:
  0.0 412.3 jit_solution(9635278765891449646)
XLA Ops:
  6.6 0.8 compare_and_fusion
  7.4 0.7 fusion.22
  8.1 0.0 dynamic-slice-start
  8.2 1.5 copy.12
  9.6 14.2 %gather_fusion = s32[4096,3]{1,0:T(8,128)} fusion(s32[3,4096]{0,1:T(8,128)S(1)} %copy.12, s32[4096]{0:T(1024)S(1)} %fusion.22), kind=kCustom, calls=%fused_computation | custom fusion | bytes 114688 | tf_op jit(solution)/shard_map/jit(_take)/gather | solution.py:72
  23.8 2.4 copy.13
  26.2 187.8 %while.12 = (s32[]{:T(128)}, f32[8,512,1,2,64]{1,0,4,3,2:T(8,128)S(1)}, f32[1024]{0:T(1024)S(1)}, s32[1]{0:T(128)}, s32[8,3,512]{2,1,0:T(4,128)S(1)}, /*index=5*...) while((s32[]{:T(128)}, ...), condition=%wide.region_1.2_spmd, body=%wide.region_0.1_spmd.sunk | while | flops 302123008 | bytes 4550849 | solution.py:67
  26.3 10.8 %fusion.36 = f32[512,128]{0,1:T(8,128)S(1)} fusion(bf16[1024,128]{0,1:T(8,128)(2,1)} %bitcast.68, s32[1024]{0:T(1024)S(1)} %bitcast.58, s32[512]{0:T(512)S(1)} %bitcast.66, s32[1024]{0:T(1024)S(1)} %bitcast.60, s32[512]{0:T(512)S(1)} %bitcast.64, s32[1024]{0:T(1024)S(1)} %bitcast.56, s32[512]{0:T(512)S(1)} %bitcast.62, s32[]{:T(128)} %bitcast.52, ...), kind=kOutput, calls=%fused_computation.14.clone.1 | convolution fusion | flops 150994944 | bytes 546820 | tf_op jit(solution)/shard_map/while/body/eval_jaxpr/dot_general | solution.py:51
  37.2 9.9 %fusion.35 = f32[512,128]{0,1:T(8,128)S(1)} fusion(bf16[1024,128]{0,1:T(8,128)(2,1)S(1)} %bitcast.69, f32[1024]{0:T(1024)S(1)} %get-tuple-element.173, s32[1024]{0:T(1024)S(1)} %bitcast.59, s32[512]{0:T(512)S(1)} %bitcast.67, s32[1024]{0:T(1024)S(1)} %bitcast.61, s32[512]{0:T(512)S(1)} %bitcast.65, s32[1024]{0:T(1024)S(1)} %bitcast.57, ...), kind=kOutput, calls=%fused_computation.15.clone.1 | convolution fusion | flops 150994944 | bytes 546820 | tf_op jit(solution)/shard_map/while/body/eval_jaxpr/dot_general | solution.py:52
  47.1 0.3 copy.20
  47.4 2.3 dynamic_update_slice.8
  49.8 10.8 %fusion.36 = f32[512,128]{0,1:T(8,128)S(1)} fusion(bf16[1024,128]{0,1:T(8,128)(2,1)} %bitcast.68, s32[1024]{0:T(1024)S(1)} %bitcast.58, s32[512]{0:T(512)S(1)} %bitcast.66, s32[1024]{0:T(1024)S(1)} %bitcast.60, s32[512]{0:T(512)S(1)} %bitcast.64, s32[1024]{0:T(1024)S(1)} %bitcast.56, s32[512]{0:T(512)S(1)} %bitcast.62, s32[]{:T(128)} %bitcast.52, ...), kind=kOutput, calls=%fused_computation.14.clone.1 | convolution fusion | flops 150994944 | bytes 546820 | tf_op jit(solution)/shard_map/while/body/eval_jaxpr/dot_general | solution.py:51
  60.6 9.9 %fusion.35 = f32[512,128]{0,1:T(8,128)S(1)} fusion(bf16[1024,128]{0,1:T(8,128)(2,1)S(1)} %bitcast.69, f32[1024]{0:T(1024)S(1)} %get-tuple-element.173, s32[1024]{0:T(1024)S(1)} %bitcast.59, s32[512]{0:T(512)S(1)} %bitcast.67, s32[1024]{0:T(1024)S(1)} %bitcast.61, s32[512]{0:T(512)S(1)} %bitcast.65, s32[1024]{0:T(1024)S(1)} %bitcast.57, ...), kind=kOutput, calls=%fused_computation.15.clone.1 | convolution fusion | flops 150994944 | bytes 546820 | tf_op jit(solution)/shard_map/while/body/eval_jaxpr/dot_general | solution.py:52
  70.6 0.3 copy.20
  70.9 2.3 dynamic_update_slice.8
  73.3 10.8 %fusion.36 = f32[512,128]{0,1:T(8,128)S(1)} fusion(bf16[1024,128]{0,1:T(8,128)(2,1)} %bitcast.68, s32[1024]{0:T(1024)S(1)} %bitcast.58, s32[512]{0:T(512)S(1)} %bitcast.66, s32[1024]{0:T(1024)S(1)} %bitcast.60, s32[512]{0:T(512)S(1)} %bitcast.64, s32[1024]{0:T(1024)S(1)} %bitcast.56, s32[512]{0:T(512)S(1)} %bitcast.62, s32[]{:T(128)} %bitcast.52, ...), kind=kOutput, calls=%fused_computation.14.clone.1 | convolution fusion | flops 150994944 | bytes 546820 | tf_op jit(solution)/shard_map/while/body/eval_jaxpr/dot_general | solution.py:51
  84.1 9.9 %fusion.35 = f32[512,128]{0,1:T(8,128)S(1)} fusion(bf16[1024,128]{0,1:T(8,128)(2,1)S(1)} %bitcast.69, f32[1024]{0:T(1024)S(1)} %get-tuple-element.173, s32[1024]{0:T(1024)S(1)} %bitcast.59, s32[512]{0:T(512)S(1)} %bitcast.67, s32[1024]{0:T(1024)S(1)} %bitcast.61, s32[512]{0:T(512)S(1)} %bitcast.65, s32[1024]{0:T(1024)S(1)} %bitcast.57, ...), kind=kOutput, calls=%fused_computation.15.clone.1 | convolution fusion | flops 150994944 | bytes 546820 | tf_op jit(solution)/shard_map/while/body/eval_jaxpr/dot_general | solution.py:52
  94.1 0.3 copy.20
  94.3 2.3 dynamic_update_slice.8
  96.7 10.8 %fusion.36 = f32[512,128]{0,1:T(8,128)S(1)} fusion(bf16[1024,128]{0,1:T(8,128)(2,1)} %bitcast.68, s32[1024]{0:T(1024)S(1)} %bitcast.58, s32[512]{0:T(512)S(1)} %bitcast.66, s32[1024]{0:T(1024)S(1)} %bitcast.60, s32[512]{0:T(512)S(1)} %bitcast.64, s32[1024]{0:T(1024)S(1)} %bitcast.56, s32[512]{0:T(512)S(1)} %bitcast.62, s32[]{:T(128)} %bitcast.52, ...), kind=kOutput, calls=%fused_computation.14.clone.1 | convolution fusion | flops 150994944 | bytes 546820 | tf_op jit(solution)/shard_map/while/body/eval_jaxpr/dot_general | solution.py:51
  107.6 9.9 %fusion.35 = f32[512,128]{0,1:T(8,128)S(1)} fusion(bf16[1024,128]{0,1:T(8,128)(2,1)S(1)} %bitcast.69, f32[1024]{0:T(1024)S(1)} %get-tuple-element.173, s32[1024]{0:T(1024)S(1)} %bitcast.59, s32[512]{0:T(512)S(1)} %bitcast.67, s32[1024]{0:T(1024)S(1)} %bitcast.61, s32[512]{0:T(512)S(1)} %bitcast.65, s32[1024]{0:T(1024)S(1)} %bitcast.57, ...), kind=kOutput, calls=%fused_computation.15.clone.1 | convolution fusion | flops 150994944 | bytes 546820 | tf_op jit(solution)/shard_map/while/body/eval_jaxpr/dot_general | solution.py:52
  117.5 0.3 copy.20
  117.8 2.3 dynamic_update_slice.8
  120.2 10.8 %fusion.36 = f32[512,128]{0,1:T(8,128)S(1)} fusion(bf16[1024,128]{0,1:T(8,128)(2,1)} %bitcast.68, s32[1024]{0:T(1024)S(1)} %bitcast.58, s32[512]{0:T(512)S(1)} %bitcast.66, s32[1024]{0:T(1024)S(1)} %bitcast.60, s32[512]{0:T(512)S(1)} %bitcast.64, s32[1024]{0:T(1024)S(1)} %bitcast.56, s32[512]{0:T(512)S(1)} %bitcast.62, s32[]{:T(128)} %bitcast.52, ...), kind=kOutput, calls=%fused_computation.14.clone.1 | convolution fusion | flops 150994944 | bytes 546820 | tf_op jit(solution)/shard_map/while/body/eval_jaxpr/dot_general | solution.py:51
  131.0 9.9 %fusion.35 = f32[512,128]{0,1:T(8,128)S(1)} fusion(bf16[1024,128]{0,1:T(8,128)(2,1)S(1)} %bitcast.69, f32[1024]{0:T(1024)S(1)} %get-tuple-element.173, s32[1024]{0:T(1024)S(1)} %bitcast.59, s32[512]{0:T(512)S(1)} %bitcast.67, s32[1024]{0:T(1024)S(1)} %bitcast.61, s32[512]{0:T(512)S(1)} %bitcast.65, s32[1024]{0:T(1024)S(1)} %bitcast.57, ...), kind=kOutput, calls=%fused_computation.15.clone.1 | convolution fusion | flops 150994944 | bytes 546820 | tf_op jit(solution)/shard_map/while/body/eval_jaxpr/dot_general | solution.py:52
  141.0 0.3 copy.20
  141.3 2.3 dynamic_update_slice.8
  143.7 10.8 %fusion.36 = f32[512,128]{0,1:T(8,128)S(1)} fusion(bf16[1024,128]{0,1:T(8,128)(2,1)} %bitcast.68, s32[1024]{0:T(1024)S(1)} %bitcast.58, s32[512]{0:T(512)S(1)} %bitcast.66, s32[1024]{0:T(1024)S(1)} %bitcast.60, s32[512]{0:T(512)S(1)} %bitcast.64, s32[1024]{0:T(1024)S(1)} %bitcast.56, s32[512]{0:T(512)S(1)} %bitcast.62, s32[]{:T(128)} %bitcast.52, ...), kind=kOutput, calls=%fused_computation.14.clone.1 | convolution fusion | flops 150994944 | bytes 546820 | tf_op jit(solution)/shard_map/while/body/eval_jaxpr/dot_general | solution.py:51
  154.5 9.9 %fusion.35 = f32[512,128]{0,1:T(8,128)S(1)} fusion(bf16[1024,128]{0,1:T(8,128)(2,1)S(1)} %bitcast.69, f32[1024]{0:T(1024)S(1)} %get-tuple-element.173, s32[1024]{0:T(1024)S(1)} %bitcast.59, s32[512]{0:T(512)S(1)} %bitcast.67, s32[1024]{0:T(1024)S(1)} %bitcast.61, s32[512]{0:T(512)S(1)} %bitcast.65, s32[1024]{0:T(1024)S(1)} %bitcast.57, ...), kind=kOutput, calls=%fused_computation.15.clone.1 | convolution fusion | flops 150994944 | bytes 546820 | tf_op jit(solution)/shard_map/while/body/eval_jaxpr/dot_general | solution.py:52
  164.5 0.3 copy.20
  164.8 2.3 dynamic_update_slice.8
  167.1 10.8 %fusion.36 = f32[512,128]{0,1:T(8,128)S(1)} fusion(bf16[1024,128]{0,1:T(8,128)(2,1)} %bitcast.68, s32[1024]{0:T(1024)S(1)} %bitcast.58, s32[512]{0:T(512)S(1)} %bitcast.66, s32[1024]{0:T(1024)S(1)} %bitcast.60, s32[512]{0:T(512)S(1)} %bitcast.64, s32[1024]{0:T(1024)S(1)} %bitcast.56, s32[512]{0:T(512)S(1)} %bitcast.62, s32[]{:T(128)} %bitcast.52, ...), kind=kOutput, calls=%fused_computation.14.clone.1 | convolution fusion | flops 150994944 | bytes 546820 | tf_op jit(solution)/shard_map/while/body/eval_jaxpr/dot_general | solution.py:51
  178.0 9.9 %fusion.35 = f32[512,128]{0,1:T(8,128)S(1)} fusion(bf16[1024,128]{0,1:T(8,128)(2,1)S(1)} %bitcast.69, f32[1024]{0:T(1024)S(1)} %get-tuple-element.173, s32[1024]{0:T(1024)S(1)} %bitcast.59, s32[512]{0:T(512)S(1)} %bitcast.67, s32[1024]{0:T(1024)S(1)} %bitcast.61, s32[512]{0:T(512)S(1)} %bitcast.65, s32[1024]{0:T(1024)S(1)} %bitcast.57, ...), kind=kOutput, calls=%fused_computation.15.clone.1 | convolution fusion | flops 150994944 | bytes 546820 | tf_op jit(solution)/shard_map/while/body/eval_jaxpr/dot_general | solution.py:52
  187.9 0.3 copy.20
  188.2 2.3 dynamic_update_slice.8
  190.6 10.8 %fusion.36 = f32[512,128]{0,1:T(8,128)S(1)} fusion(bf16[1024,128]{0,1:T(8,128)(2,1)} %bitcast.68, s32[1024]{0:T(1024)S(1)} %bitcast.58, s32[512]{0:T(512)S(1)} %bitcast.66, s32[1024]{0:T(1024)S(1)} %bitcast.60, s32[512]{0:T(512)S(1)} %bitcast.64, s32[1024]{0:T(1024)S(1)} %bitcast.56, s32[512]{0:T(512)S(1)} %bitcast.62, s32[]{:T(128)} %bitcast.52, ...), kind=kOutput, calls=%fused_computation.14.clone.1 | convolution fusion | flops 150994944 | bytes 546820 | tf_op jit(solution)/shard_map/while/body/eval_jaxpr/dot_general | solution.py:51
  201.4 9.9 %fusion.35 = f32[512,128]{0,1:T(8,128)S(1)} fusion(bf16[1024,128]{0,1:T(8,128)(2,1)S(1)} %bitcast.69, f32[1024]{0:T(1024)S(1)} %get-tuple-element.173, s32[1024]{0:T(1024)S(1)} %bitcast.59, s32[512]{0:T(512)S(1)} %bitcast.67, s32[1024]{0:T(1024)S(1)} %bitcast.61, s32[512]{0:T(512)S(1)} %bitcast.65, s32[1024]{0:T(1024)S(1)} %bitcast.57, ...), kind=kOutput, calls=%fused_computation.15.clone.1 | convolution fusion | flops 150994944 | bytes 546820 | tf_op jit(solution)/shard_map/while/body/eval_jaxpr/dot_general | solution.py:52
  211.4 0.3 copy.20
  211.7 2.3 dynamic_update_slice.8
  214.0 4.4 %reshape_reshape_reshape.3 = f32[32,2,64,1,2,64]{2,1,0,5,4,3:T(2,128)} reshape(f32[8,512,1,2,64]{1,0,4,3,2:T(8,128)S(1)} %get-tuple-element.95) | data formatting | bytes 4194304 | tf_op jit(solution)/shard_map/reshape;reshape;reshape | solution.py:16
  218.4 7.3 %copy.15 = f32[2,32,64,1,2,64]{5,2,4,3,1,0:T(8,128)} copy(f32[2,32,64,1,2,64]{2,0,1,5,4,3:T(2,128)} %bitcast.54) | data formatting | bytes 4194304 | tf_op jit(solution)/shard_map/transpose | solution.py:17
  225.7 0.1 reduce-scatter.3.cloned.1.call-update
  225.7 0.1 reduce-scatter.5.cloned.1.call-start
  225.8 40.7 %reduce-scatter.3.cloned.1.call-done = f32[32,64,1,2,64]{4,1,3,2,0:T(8,128)} async-done(((f32[64,64,1,2,64]{4,1,3,2,0:T(8,128)}), f32[32,64,1,2,64]{4,1,3,2,0:T(8,128)}) %reduce-scatter.3.cloned.1.call-update) | async-done | bytes 1048592 | tf_op jit(solution)/shard_map/reduce_scatter | solution.py:20
  266.5 0.1 reduce-scatter.5.cloned.1.call-update
  266.6 137.4 %reduce-scatter.5.cloned.1.call-done = f32[1,64,1,2,64]{4,1,3,2,0:T(8,128)} async-done(((f32[32,64,1,2,64]{4,1,3,2,0:T(8,128)}), f32[1,64,1,2,64]{4,1,3,2,0:T(8,128)}) %reduce-scatter.5.cloned.1.call-update) | async-done | bytes 32784 | tf_op jit(solution)/shard_map/reduce_scatter | solution.py:20
  404.0 0.8 convert_bitcast_fusion
  404.8 0.6 copy.16
  (66 shorter events, 0.8 us)
Async XLA Ops:
  6.5 1.6 copy-start
  6.6 260.0 %reduce-scatter.3.cloned.1.call-start = ((), (), s32[]{:S(2)}) async-start(), calls=%async_computation.2 | async-start | bytes 6291456 | tf_op jit(solution)/shard_map/reduce_scatter | solution.py:20
  8.1 18.1 %dynamic-slice-start = ((f32[65536]{0:T(1024)}, s32[]{:T(128)}), f32[1024]{0:T(1024)S(1)}, s32[]{:S(2)}) async-start(f32[65536]{0:T(1024)} %param.12, s32[]{:T(128)} %select_n.33), calls=%async_computation.4 | async-start | bytes 8704 | tf_op jit(solution)/shard_map/dynamic_slice | solution.py:77
  23.8 2.4 copy-start.1
  26.3 10.8 %copy-start.2 = (bf16[1,1024,2,64]{1,3,2,0:T(8,128)(2,1)S(1)}, bf16[1,1024,2,64]{1,3,2,0:T(8,128)(2,1)}, u32[]{:S(2)}) copy-start(bf16[1,1024,2,64]{1,3,2,0:T(8,128)(2,1)} %get-tuple-element.211) | copy-start | bytes 786436 | tf_op jit(solution)/shard_map/while
  49.8 10.8 %copy-start.2 = (bf16[1,1024,2,64]{1,3,2,0:T(8,128)(2,1)S(1)}, bf16[1,1024,2,64]{1,3,2,0:T(8,128)(2,1)}, u32[]{:S(2)}) copy-start(bf16[1,1024,2,64]{1,3,2,0:T(8,128)(2,1)} %get-tuple-element.211) | copy-start | bytes 786436 | tf_op jit(solution)/shard_map/while
  73.2 10.8 %copy-start.2 = (bf16[1,1024,2,64]{1,3,2,0:T(8,128)(2,1)S(1)}, bf16[1,1024,2,64]{1,3,2,0:T(8,128)(2,1)}, u32[]{:S(2)}) copy-start(bf16[1,1024,2,64]{1,3,2,0:T(8,128)(2,1)} %get-tuple-element.211) | copy-start | bytes 786436 | tf_op jit(solution)/shard_map/while
  96.7 10.8 %copy-start.2 = (bf16[1,1024,2,64]{1,3,2,0:T(8,128)(2,1)S(1)}, bf16[1,1024,2,64]{1,3,2,0:T(8,128)(2,1)}, u32[]{:S(2)}) copy-start(bf16[1,1024,2,64]{1,3,2,0:T(8,128)(2,1)} %get-tuple-element.211) | copy-start | bytes 786436 | tf_op jit(solution)/shard_map/while
  120.2 10.8 %copy-start.2 = (bf16[1,1024,2,64]{1,3,2,0:T(8,128)(2,1)S(1)}, bf16[1,1024,2,64]{1,3,2,0:T(8,128)(2,1)}, u32[]{:S(2)}) copy-start(bf16[1,1024,2,64]{1,3,2,0:T(8,128)(2,1)} %get-tuple-element.211) | copy-start | bytes 786436 | tf_op jit(solution)/shard_map/while
  143.7 10.8 %copy-start.2 = (bf16[1,1024,2,64]{1,3,2,0:T(8,128)(2,1)S(1)}, bf16[1,1024,2,64]{1,3,2,0:T(8,128)(2,1)}, u32[]{:S(2)}) copy-start(bf16[1,1024,2,64]{1,3,2,0:T(8,128)(2,1)} %get-tuple-element.211) | copy-start | bytes 786436 | tf_op jit(solution)/shard_map/while
  167.1 10.8 %copy-start.2 = (bf16[1,1024,2,64]{1,3,2,0:T(8,128)(2,1)S(1)}, bf16[1,1024,2,64]{1,3,2,0:T(8,128)(2,1)}, u32[]{:S(2)}) copy-start(bf16[1,1024,2,64]{1,3,2,0:T(8,128)(2,1)} %get-tuple-element.211) | copy-start | bytes 786436 | tf_op jit(solution)/shard_map/while
  190.6 10.8 %copy-start.2 = (bf16[1,1024,2,64]{1,3,2,0:T(8,128)(2,1)S(1)}, bf16[1,1024,2,64]{1,3,2,0:T(8,128)(2,1)}, u32[]{:S(2)}) copy-start(bf16[1,1024,2,64]{1,3,2,0:T(8,128)(2,1)} %get-tuple-element.211) | copy-start | bytes 786436 | tf_op jit(solution)/shard_map/while
  225.7 178.3 %reduce-scatter.5.cloned.1.call-start = ((), (), s32[]{:S(2)}) async-start(), calls=%async_computation.3 | async-start | bytes 2162688 | tf_op jit(solution)/shard_map/reduce_scatter | solution.py:20
Sparse Core Ops, SparseCore 0:
  225.9 40.6 reduce-scatter.2
  269.1 134.8 reduce-scatter.4
where the time goes:
time: 413 us; the launch traced here: 412 us
  waiting for transfers between devices  178 us (43%)
  matrix products  166 us (40%)
  local copies, waits for them, and re-layouts  51.1 us (12%)
  between operations  13.5 us (3%)
    reduce_scatter x2, waiting for transfers between devices, sum_in_order(): pieces = lax.psum_scatter(pieces, axes[k], scatter_dimension=0, tiled=True)  178 us
    dot_general x8, matrix products, beam_terms(): with_real = jnp.dot(weight_re, columns, preferred_element_type=jnp.float32)  86.5 us
    dot_general x8, matrix products, beam_terms(): with_imag = jnp.dot(weight_im, columns, preferred_element_type=jnp.float32)  79.2 us
    dynamic_update_slice x16, local copies, waits for them, and re-layouts, blocked_terms(): result = lax.map(per_block, blocks)  20.5 us
    gather x2, local copies, waits for them, and re-layouts, per_device(): ordered = jnp.take(directions, beam_order, axis=1)  16.5 us
  transfers between devices with their start and end apart: 2, of which 2 were waited for; matrix products, arithmetic and copies ran while one was open for 0% of the time, Pallas kernels for 0%

commit v1 on v0

v1 whole, which is shorter than its diff:
```python
import functools
import math

import jax
import jax.numpy as jnp
from jax import lax
from jax.experimental import pallas as pl
from jax.experimental.pallas import tpu as pltpu
from jax.sharding import PartitionSpec as P

CYCLE = 8192
CORES = 2
NEAR = 4
F32 = jnp.float32
BF16 = jnp.bfloat16
SIN = (4.442867903016298, -7.3074434206684415, 3.594788072467163, -0.7843740145897882)
COS = (-1.4142040805466873, 6.977642058572177, -5.7152384030951175, 1.7283486671441728)


def poly(coefs, z):
    total = coefs[-1]
    for coef in coefs[-2::-1]:
        total = total * z + coef
    return total


def centred(value, period):
    return ((value + period // 2) & (period - 1)) - period // 2


def beam_features(core, bin_value, dirs, order, feat, near):
    chips = order.shape[0]
    far = chips // near
    steps = centred(bin_value * dirs[...], CYCLE)
    high = (steps + 32) >> 6
    low = steps - (high << 6)
    shift = (steps[0:1] + steps[1:2] + steps[2:3]) & 31
    terms = [high.astype(F32) * (64.0 / CYCLE), low.astype(F32) * (1.0 / CYCLE), shift.astype(F32) * (256.0 / CYCLE)]
    terms = jnp.concatenate([*terms, jnp.zeros(shift.shape, F32)], axis=0)
    tiles = terms.shape[1] // 128
    table = jnp.concatenate([terms[:, 128 * q : 128 * q + 128] for q in range(tiles)], axis=0).astype(BF16)
    lane = lax.broadcasted_iota(jnp.int32, (1, 128), 1)
    sub = lax.broadcasted_iota(jnp.int32, (128, 128), 0)
    for t in range(chips // 2):
        rows = []
        for j in (2 * t, 2 * t + 1):
            chip = near * (j % far) + j // far
            rows.append(order[chip : chip + 1, :])
        first = jnp.where(core == 0, rows[0], pltpu.roll(rows[0], 64, 1))
        second = jnp.where(core == 0, pltpu.roll(rows[1], 64, 1), rows[1])
        beam = jnp.where(lane < 64, first, second)
        hot = jnp.where(sub == (beam & 127), 1.0, 0.0).astype(BF16)
        picked = jnp.dot(table, hot, preferred_element_type=F32)
        which = beam >> 7
        total = jnp.zeros((8, 128), F32)
        for q in range(tiles):
            total = jnp.where(which == q, picked[8 * q : 8 * q + 8], total)
        feat[128 * t : 128 * t + 128, :] = total.T.astype(BF16)


def weights_kernel(scal, xs0, xs1, pos0, pos1, tap0, tap1, dirs, order, out, feat, place, turned, *, near, tb, te, elem):
    beam_features(scal[1], scal[2], dirs, order, feat, near)
    parts = []
    for k, (xs, pos, tap) in enumerate(((xs0, pos0, tap0), (xs1, pos1, tap1))):
        where = (pos[...] - 256).astype(F32)
        one = jnp.ones((1, where.shape[1]), F32)
        place[k] = jnp.concatenate([where, where, one, one * 0.0], axis=0).astype(BF16)
        half = xs.shape[0] // 2
        turned[k, :half] = -xs[half:]
        turned[k, half:] = xs[:half]
        parts.append((xs, tap[...] * (1.0 / math.sqrt(elem))))
    contract = (((1,), (1,)), ((), ()))

    def step(i, carry):
        at = pl.multiple_of(i * tb, tb)
        beams = feat[pl.ds(at, tb), :]
        total = jnp.zeros((tb, out.shape[1]), F32)
        for k, (xs, amplitude) in enumerate(parts):
            for e in range(0, xs.shape[1], te):
                cols = slice(e, e + te)
                turns = jnp.dot(beams, place[k, :, cols], preferred_element_type=F32)
                r = turns - jnp.round(turns)
                z = r * r
                s = r * poly(SIN, z)
                a = amplitude[:, cols]
                scaled = a * s
                weight_re = (a - scaled * s).astype(BF16)
                weight_im = (scaled * poly(COS, z)).astype(BF16)
                total += lax.dot_general(weight_re, xs[:, cols], contract, preferred_element_type=F32)
                total += lax.dot_general(weight_im, turned[k, :, cols], contract, preferred_element_type=F32)
        out[pl.ds(at, tb), :] = total.astype(out.dtype)
        return carry

    lax.fori_loop(0, out.shape[0] // tb, step, 0)


def partial_beams(scal, mine, other, positions, taper, directions, order, near):
    cols, count = mine.shape
    elem = positions.shape[1]
    beams = directions.shape[1] // CORES
    own = lambda i, s: (0, s[0])
    mate = lambda i, s: (0, s[0] + 1 - 2 * s[1])
    whole = lambda i, s: (0, 0)
    kernel = functools.partial(weights_kernel, near=near, tb=128, te=256, elem=elem)
    return pl.pallas_call(
        kernel,
        grid_spec=pltpu.PrefetchScalarGridSpec(
            num_scalar_prefetch=1,
            grid=(1,),
            in_specs=[
                pl.BlockSpec((cols, count), whole),
                pl.BlockSpec((cols, count), whole),
                pl.BlockSpec((3, count), own),
                pl.BlockSpec((3, count), mate),
                pl.BlockSpec((1, count), own),
                pl.BlockSpec((1, count), mate),
                pl.BlockSpec(directions.shape, whole),
                pl.BlockSpec(order.shape, whole),
            ],
            out_specs=pl.BlockSpec((beams, cols), whole),
            scratch_shapes=[
                pltpu.VMEM((beams, 8), BF16),
                pltpu.VMEM((2, 8, count), BF16),
                pltpu.VMEM((2, cols, count), BF16),
            ],
        ),
        out_shape=jax.ShapeDtypeStruct((beams, cols), BF16),
        name="weights",
    )(scal, mine, other, positions, positions, taper, taper, directions, order)


def per_device(snapshots, bin_index, positions, directions, taper, beam_order):
    blocks = lax.axis_size("blk")
    chips = blocks // CORES
    far = chips // NEAR
    count = snapshots.shape[1]
    cols = snapshots.shape[2] * snapshots.shape[3]
    index = lax.axis_index("blk")
    core = index % CORES
    mine = snapshots[0].transpose(1, 2, 0).reshape(cols, count)
    other = lax.ppermute(mine, "blk", [(i, i ^ 1) for i in range(blocks)])
    scal = jnp.stack([index, core, bin_index[0]]).astype(jnp.int32)
    order = beam_order.reshape(chips, -1)
    sums = partial_beams(scal, mine, other, positions, taper[None], directions, order, NEAR)
    owned = sums.shape[0] // chips
    near_groups = [[CORES * (j * NEAR + i) + c for i in range(NEAR)] for j in range(far) for c in range(CORES)]
    far_groups = [[CORES * (i * NEAR + j) + c for i in range(far)] for j in range(NEAR) for c in range(CORES)]
    sums = sums.reshape(NEAR, far * owned, cols)
    sums = lax.all_to_all(sums, "blk", 0, 0, axis_index_groups=near_groups, tiled=True)
    sums = sums.astype(F32).sum(0).astype(BF16).reshape(far, owned, cols)
    sums = lax.all_to_all(sums, "blk", 0, 0, axis_index_groups=far_groups, tiled=True)
    sums = sums.astype(F32).sum(0).astype(BF16)
    return sums.reshape(owned, 1, snapshots.shape[2], snapshots.shape[3])


def solution(mesh):
    return jax.shard_map(
        per_device,
        mesh=mesh,
        in_specs=(P("groups", "blk", None, None), P("groups"), P(), P(), P(), P()),
        out_specs=P("blk", "groups", None, None),
        check_vma=False,
    )
```

time: 413 us -> 106 us (0.26)
  waiting for transfers between devices: 178 us -> 0.44 us
  matrix products: 166 us -> 0 us
  blocking collectives: 0 us -> 78.3 us
  local copies, waits for them, and re-layouts: 51.1 us -> 1.4 us
  Pallas kernels: 0 us -> 24.1 us
  between operations: 13.5 us -> 0.66 us
    reduce_scatter x2 -> x0, waiting for transfers between devices: 178 us -> none  [sum_in_order(): pieces = lax.psum_scatter(pieces, axes[k], scatter_dimension=0, tiled=True)]
    dot_general x16 -> x0, matrix products: 166 us -> none  [the longest x8 86.5 us: beam_terms(): with_real = jnp.dot(weight_re, columns, preferred_element_type=jnp.float32)]
    all_to_all x0 -> x2, blocking collectives: none -> 78.3 us  [the longest x1 57 us: per_device(): lax.all_to_all(sums, 'blk', 0, 0, axis_index_groups=far_groups, tiled=True)]
    pallas_call x0 -> x1, Pallas kernels: none -> 24.1 us  [partial_beams(): pl.pallas_call(kernel, grid_spec=pltpu.PrefetchScalarGridSpec(num_scalar_...]
    dynamic_update_slice x16 -> x0, local copies, waits for them, and re-layouts: 20.5 us -> none  [blocked_terms(): result = lax.map(per_block, blocks)]
    gather x2 -> x0, local copies, waits for them, and re-layouts: 16.5 us -> none  [per_device(): ordered = jnp.take(directions, beam_order, axis=1)]
    transpose x1 -> x0, local copies, waits for them, and re-layouts: 7.29 us -> none  [sum_in_order(): pieces = pieces.transpose(*sequence, *range(len(axes), pieces.ndim))]
    another operation x1 -> x0, local copies, waits for them, and re-layouts: 4.39 us -> none  [sum_in_order(): pieces = pieces.reshape(*lengths, *pieces.shape[1:])]
  transfers between devices with their start and end apart: 2 -> 1, of which waited for: 2 -> 1; matrix products, arithmetic and copies ran while one was open for 0% -> 1% of each run, Pallas kernels for 0% -> 0%
where the time goes in v1:
time: 106 us
  blocking collectives  78.3 us (74%)
  Pallas kernels  24.1 us (23%)
  local copies, waits for them, and re-layouts  1.4 us (1%)
    all_to_all x1, blocking collectives, per_device(): lax.all_to_all(sums, 'blk', 0, 0, axis_index_groups=far_groups, tiled=True)  57 us
    pallas_call x1, Pallas kernels, partial_beams(): pl.pallas_call(kernel, grid_spec=pltpu.PrefetchScalarGridSpec(num_scalar_...  24.1 us
    all_to_all x1, blocking collectives, per_device(): lax.all_to_all(sums, 'blk', 0, 0, axis_index_groups=near_groups, tiled=True)  21.3 us
  transfers between devices with their start and end apart: 1, of which 1 were waited for; matrix products, arithmetic and copies ran while one was open for 1% of the time, Pallas kernels for 0%

profile of v1, /device:TPU:38, one launch (start us, length us, event | category | flops | bytes accessed | tf_op | source)
XLA Modules:
  0.0 105.6 jit_solution(17774575923401703471)
XLA Ops:
  0.0 0.0 collective-permute-start
  0.7 0.7 pad_add_fusion.scal
  1.3 0.4 collective-permute-done.xs1
  1.7 0.0 copy-start
  1.7 0.7 copy-done
  2.5 24.1 %weights.1 = bf16[2048,128]{1,0:T(8,128)(2,1)} custom-call(s32[3]{0:T(128)} %pad_add_fusion.scal, bf16[128,1024]{1,0:T(8,128)(2,1)} %bitcast.17, bf16[128,1024]{1,0:T(8,128)(2,1)} %copy-done, s32[3,65536]{1,0:T(4,128)} %pos1.1, s32[3,65536]{1,0:T(4,128)} %pos1.1, f32[1,65536]{1,0:T(1,128)} %bitcast.13, f32[1,65536]{1,0:T(1,128)} %bitcast.14, ...), custom_call_target="tpu_custom_call" | custom-call | tf_op jit(solution)/shard_map/weights/pallas_call | solution.py:105
  26.5 21.3 %all_to_all.10 = bf16[4,512,128]{2,1,0:T(8,128)(2,1)S(1)} all-to-all(bf16[4,512,128]{2,1,0:T(8,128)(2,1)} %bitcast.12), channel_id=1, replica_groups={{0,2,4,6},{1,3,5,7},{8,10,12,14},{9,11,13,15},{16,18,20,22},{17,19,21,2..., dimensions={0} | all-to-all | bytes 1048576 | tf_op jit(solution)/shard_map/all_to_all | solution.py:149
  47.8 0.1 reduce_sum.24
  47.9 57.0 %all_to_all.11 = bf16[8,64,128]{2,1,0:T(8,128)(2,1)S(1)} all-to-all(bf16[8,64,128]{2,1,0:T(8,128)(2,1)S(1)} %bitcast.15), channel_id=1, replica_groups={{0,8,16,24,32,40,48,56},{1,9,17,25,33,41,49,57},{2,10,18,26,34,42,50,58..., dimensions={0} | all-to-all | bytes 262144 | tf_op jit(solution)/shard_map/all_to_all | solution.py:151
  104.9 0.7 reshape.19
  (1 shorter events, 0.0 us)
Async XLA Ops:
  0.0 1.7 %collective-permute-start = (bf16[128,1024]{1,0:T(8,128)(2,1)}, bf16[128,1024]{1,0:T(8,128)(2,1)S(1)}, u32[]{:S(2)}, u32[]{:S(2)}) collective-permute-start(bf16[128,1024]{1,0:T(8,128)(2,1)} %bitcast.16), channel_id=1, source_target_pairs={{0,1},{1,0},{2,3},{3,2},{4,5},{5,4},{6,7},{7,6},{8,9},{9,8},{10,11... | collective-permute-start | bytes 786440 | tf_op jit(solution)/shard_map/ppermute | solution.py:141
  1.7 0.7 copy-start

commit v2 on v1

v2 whole, which is shorter than its diff:
```python
import functools
import math

import jax
import jax.numpy as jnp
from jax import lax
from jax.experimental import pallas as pl
from jax.experimental.pallas import tpu as pltpu
from jax.sharding import PartitionSpec as P

CYCLE = 8192
CORES = 2
NEAR = 4
CUTS = (4,)
TB = 1024
TE = 256
F32 = jnp.float32
BF16 = jnp.bfloat16
SIN = (4.442867903016298, -7.3074434206684415, 3.594788072467163, -0.7843740145897882)
COS = (-1.4142040805466873, 6.977642058572177, -5.7152384030951175, 1.7283486671441728)


def split_cubic(coefs):
    lead = coefs[3]
    a, b = coefs[2] / lead, coefs[1] / lead
    return lead, a, b, coefs[0] / lead - a * b


def centred(value, period):
    return ((value + period // 2) & (period - 1)) - period // 2


def beam_features(core, bin_value, dirs, order, feat, near, first, last):
    span = last - first
    steps = centred(bin_value * dirs[...], CYCLE)
    high = (steps + 32) >> 6
    low = steps - (high << 6)
    shift = (steps[0:1] + steps[1:2] + steps[2:3]) & 31
    terms = [high.astype(F32) * (64.0 / CYCLE), low.astype(F32) * (1.0 / CYCLE), shift.astype(F32) * (256.0 / CYCLE)]
    terms = jnp.concatenate([*terms, jnp.zeros(shift.shape, F32)], axis=0)
    tiles = terms.shape[1] // 128
    table = jnp.concatenate([terms[:, 128 * q : 128 * q + 128] for q in range(tiles)], axis=0).astype(BF16)
    lane = lax.broadcasted_iota(jnp.int32, (1, 128), 1)
    sub = lax.broadcasted_iota(jnp.int32, (128, 128), 0)
    for t in range(near * span // 2):
        rows = []
        for j in (2 * t, 2 * t + 1):
            chip = near * (first + j % span) + j // span
            rows.append(order[chip : chip + 1, :])
        left = jnp.where(core == 0, rows[0], pltpu.roll(rows[0], 64, 1))
        right = jnp.where(core == 0, pltpu.roll(rows[1], 64, 1), rows[1])
        beam = jnp.where(lane < 64, left, right)
        hot = jnp.where(sub == (beam & 127), 1.0, 0.0).astype(BF16)
        picked = jnp.dot(table, hot, preferred_element_type=F32)
        which = beam >> 7
        total = jnp.zeros((8, 128), F32)
        for q in range(tiles):
            total = jnp.where(which == q, picked[8 * q : 8 * q + 8], total)
        feat[128 * t : 128 * t + 128, :] = total.T.astype(BF16)


def weights_kernel(bins, mine, other, positions, taper, dirs, order, out, feat, place, turned, pos, tap, sems, *, near, first, last, tb, te):
    index = lax.axis_index("blk")
    core = index % CORES
    count = mine.shape[1]
    copies = []
    for k, owner in enumerate((index, index + 1 - 2 * core)):
        at = pl.ds(pl.multiple_of(owner * count, count), count)
        copies.append(pltpu.make_async_copy(positions.at[:, at], pos.at[k], sems.at[0, k]))
        copies.append(pltpu.make_async_copy(taper.at[:, at], tap.at[k], sems.at[1, k]))
    for copy in copies:
        copy.start()
    beam_features(core, bins[0], dirs, order, feat, near, first, last)
    for copy in copies:
        copy.wait()
    sin_lead, sin_a, sin_b, sin_c = split_cubic(SIN)
    cos_lead, cos_a, cos_b, cos_c = split_cubic(COS)
    ratio = cos_lead / sin_lead
    parts = []
    for k, xs in enumerate((mine, other)):
        where = (pos[k] - 256).astype(F32)
        one = jnp.ones((1, count), F32)
        place[k] = jnp.concatenate([where, where, one, one * 0.0], axis=0).astype(BF16)
        half = xs.shape[0] // 2
        turned[k, :half] = -xs[half:]
        turned[k, half:] = xs[:half]
        amplitude = tap[k] * (1.0 / math.sqrt(taper.shape[1]))
        parts.append((xs, amplitude, amplitude * (sin_lead * sin_lead)))
    contract = (((1,), (1,)), ((), ()))

    def step(i, carry):
        at = pl.multiple_of(i * tb, tb)
        beams = feat[pl.ds(at, tb), :]
        total = jnp.zeros((tb, out.shape[1]), F32)
        for k, (xs, amplitude, doubled) in enumerate(parts):
            for e in range(0, count, te):
                cols = slice(e, e + te)
                turns = jnp.dot(beams, place[k, :, cols], preferred_element_type=F32)
                r = turns - jnp.round(turns)
                z = r * r
                w = z * z
                t = r * ((z + sin_a) * (w + sin_b) + sin_c)
                scaled = doubled[:, cols] * t
                weight_re = (amplitude[:, cols] - scaled * t).astype(BF16)
                weight_im = (scaled * ((ratio * z + ratio * cos_a) * (w + cos_b) + ratio * cos_c)).astype(BF16)
                total += lax.dot_general(weight_re, xs[:, cols], contract, preferred_element_type=F32)
                total += lax.dot_general(weight_im, turned[k, :, cols], contract, preferred_element_type=F32)
        out[pl.ds(at, tb), :] = total.astype(out.dtype)
        return carry

    lax.fori_loop(0, out.shape[0] // tb, step, 0)


def partial_beams(bins, mine, other, positions, taper, directions, order, near, first, last):
    cols, count = mine.shape
    beams = near * (last - first) * order.shape[1] // CORES
    kernel = functools.partial(weights_kernel, near=near, first=first, last=last, tb=math.gcd(TB, beams), te=TE)
    vmem = pl.BlockSpec(memory_space=pltpu.VMEM)
    hbm = pl.BlockSpec(memory_space=pl.ANY)
    return pl.pallas_call(
        kernel,
        in_specs=[pl.BlockSpec(memory_space=pltpu.SMEM), vmem, vmem, hbm, hbm, vmem, vmem],
        out_specs=vmem,
        scratch_shapes=[
            pltpu.VMEM((beams, 8), BF16),
            pltpu.VMEM((2, 8, count), BF16),
            pltpu.VMEM((2, cols, count), BF16),
            pltpu.VMEM((2, 3, count), jnp.int32),
            pltpu.VMEM((2, 1, count), F32),
            pltpu.SemaphoreType.DMA((2, 2)),
        ],
        out_shape=jax.ShapeDtypeStruct((beams, cols), BF16),
        cost_estimate=pl.CostEstimate(flops=beams * count * cols * 8, bytes_accessed=2 * cols * count * 4, transcendentals=0),
        name=f"weights_{first}",
    )(bins, mine, other, positions, taper, directions, order)


def per_device(snapshots, bin_index, positions, directions, taper, beam_order):
    blocks = lax.axis_size("blk")
    chips = blocks // CORES
    far = chips // NEAR
    owned = beam_order.shape[0] // blocks
    count = snapshots.shape[1]
    cols = snapshots.shape[2] * snapshots.shape[3]
    mine = snapshots[0].transpose(1, 2, 0).reshape(cols, count)
    other = pltpu.with_memory_space_constraint(lax.ppermute(mine, "blk", [(i, i ^ 1) for i in range(blocks)]), pltpu.VMEM)
    order = beam_order.reshape(chips, -1)
    near_groups = [[CORES * (j * NEAR + i) + c for i in range(NEAR)] for j in range(far) for c in range(CORES)]
    far_groups = [[CORES * (i * NEAR + j) + c for i in range(far)] for j in range(NEAR) for c in range(CORES)]
    cuts = [0, *(far * c // 8 for c in CUTS), far]
    pieces = []
    for k, (first, last) in enumerate(zip(cuts[:-1], cuts[1:])):
        with jax.named_scope(f"weigh_{k}"):
            sums = partial_beams(bin_index, mine, other, positions, taper[None], directions, order, NEAR, first, last)
        with jax.named_scope(f"near_{k}"):
            sums = lax.all_to_all(sums.reshape(NEAR, -1, cols), "blk", 0, 0, axis_index_groups=near_groups, tiled=True)
        pieces.append(sums.astype(F32).sum(0).astype(BF16).reshape(last - first, owned, cols))
    sums = jnp.concatenate(pieces, axis=0)
    sums = lax.all_to_all(sums, "blk", 0, 0, axis_index_groups=far_groups, tiled=True)
    sums = sums.astype(F32).sum(0).astype(BF16)
    return sums.reshape(owned, 1, snapshots.shape[2], snapshots.shape[3])


def solution(mesh):
    return jax.shard_map(
        per_device,
        mesh=mesh,
        in_specs=(P("groups", "blk", None, None), P("groups"), P(), P(), P(), P()),
        out_specs=P("blk", "groups", None, None),
        check_vma=False,
    )
```

time: 106 us -> 96.6 us (0.911)
  blocking collectives: 78.3 us -> 55.1 us
  starting transfers between devices: 0.01 us -> 11.5 us
  waiting for transfers between devices: 0.44 us -> 9.77 us
  Pallas kernels: 24.1 us -> 18.2 us
    all_to_all x1 -> x0, blocking collectives: 21.3 us -> none  [per_device(): lax.all_to_all(sums, 'blk', 0, 0, axis_index_groups=near_groups, tiled=True)]
    all_to_all x0 -> x2, starting transfers between devices: none -> 11.5 us  [per_device(): lax.all_to_all(sums.reshape(NEAR, -1, cols), 'blk', 0, 0, axis_index_grou...]
    all_to_all x0 -> x2, waiting for transfers between devices: none -> 8.68 us  [per_device(): lax.all_to_all(sums.reshape(NEAR, -1, cols), 'blk', 0, 0, axis_index_grou...]
    pallas_call x1 -> x2, Pallas kernels: 24.1 us -> 18.2 us  [partial_beams(): pl.pallas_call(kernel, in_specs=[pl.BlockSpec(memory_space=pltpu.SMEM), v...]
    all_to_all x1, blocking collectives: 57 us -> 55.1 us  [per_device(): lax.all_to_all(sums, 'blk', 0, 0, axis_index_groups=far_groups, tiled=True)]
  transfers between devices with their start and end apart: 1 -> 3, of which waited for: 1 -> 3; matrix products, arithmetic and copies ran while one was open for 1% -> 0% of each run, Pallas kernels for 0% -> 9%
where the time goes in v2:
time: 96.6 us; the launch traced here: 96.1 us
  blocking collectives  55.1 us (57%)
  Pallas kernels  18.2 us (19%)
  starting transfers between devices  11.5 us (12%)
  waiting for transfers between devices  9.77 us (10%)
    all_to_all x1, blocking collectives, per_device(): lax.all_to_all(sums, 'blk', 0, 0, axis_index_groups=far_groups, tiled=True)  55.1 us
    pallas_call x2, Pallas kernels, partial_beams(): pl.pallas_call(kernel, in_specs=[pl.BlockSpec(memory_space=pltpu.SMEM), v...  18.2 us
    all_to_all x2, starting transfers between devices, per_device(): lax.all_to_all(sums.reshape(NEAR, -1, cols), 'blk', 0, 0, axis_index_grou...  11.5 us
    all_to_all x2, waiting for transfers between devices, per_device(): lax.all_to_all(sums.reshape(NEAR, -1, cols), 'blk', 0, 0, axis_index_grou...  8.68 us
  transfers between devices with their start and end apart: 3, of which 3 were waited for; matrix products, arithmetic and copies ran while one was open for 0% of the time, Pallas kernels for 9%

profile of v2, /device:TPU:38, one launch (start us, length us, event | category | flops | bytes accessed | tf_op | source)
XLA Modules:
  0.0 96.1 jit_solution(632213405462542297)
XLA Ops:
  0.0 0.0 collective-permute-start
  0.7 1.1 %collective-permute-done.other = bf16[128,1024]{1,0:T(8,128)(2,1)S(1)} collective-permute-done((bf16[128,1024]{1,0:T(8,128)(2,1)}, bf16[128,1024]{1,0:T(8,128)(2,1)S(1)}, u32[]{:S(2)}, u32[]{:S(2)}) %collective-permute-start) | collective-permute-done | bytes 262176 | tf_op jit(solution)/shard_map/ppermute | solution.py:146
  1.7 9.1 %weights_4.1 = bf16[1024,128]{1,0:T(8,128)(2,1)} custom-call(s32[1]{0:T(128)S(6)} %copy.8.bins, bf16[128,1024]{1,0:T(8,128)(2,1)} %bitcast.17, bf16[128,1024]{1,0:T(8,128)(2,1)S(1)} %collective-permute-done.other, s32[3,65536]{1,0:T(4,128)} %positions.3, f32[1,65536]{1,0:T(1,128)} %bitcast.19, s32[3,4096]{1,0:T(4,128)} %dirs.3, s32[32,128]{1,0:T(8,128)} %bitcast.21), custom_call_target="tpu_custom_call" | custom-call | flops 1073741824 | bytes 1048576 | tf_op jit(solution)/shard_map/weigh_1/weights_4/pallas_call | solution.py:120
  10.8 6.5 %all-to-all-start.1 = ((bf16[4,256,128]{2,1,0:T(8,128)(2,1)}), bf16[4,256,128]{2,1,0:T(8,128)(2,1)S(1)}, u32[]{:S(2)}, u32[]{:S(2)}) async-start(bf16[4,256,128]{2,1,0:T(8,128)(2,1)} %bitcast.13), calls=%async_computation.1 | async-start | bytes 524288 | tf_op jit(solution)/shard_map/near_1/all_to_all | solution.py:156
  17.4 9.1 %weights_0.1 = bf16[1024,128]{1,0:T(8,128)(2,1)} custom-call(s32[1]{0:T(128)S(6)} %copy.8.bins, bf16[128,1024]{1,0:T(8,128)(2,1)} %bitcast.18, bf16[128,1024]{1,0:T(8,128)(2,1)S(1)} %collective-permute-done.other, s32[3,65536]{1,0:T(4,128)} %positions.3, f32[1,65536]{1,0:T(1,128)} %bitcast.20, s32[3,4096]{1,0:T(4,128)} %dirs.3, s32[32,128]{1,0:T(8,128)} %bitcast.22), custom_call_target="tpu_custom_call" | custom-call | flops 1073741824 | bytes 1048576 | tf_op jit(solution)/shard_map/weigh_0/weights_0/pallas_call | solution.py:120
  26.5 0.1 all-to-all-done.1
  26.6 5.0 %all-to-all-start = ((bf16[4,256,128]{2,1,0:T(8,128)(2,1)}), bf16[4,256,128]{2,1,0:T(8,128)(2,1)S(1)}, u32[]{:S(2)}, u32[]{:S(2)}) async-start(bf16[4,256,128]{2,1,0:T(8,128)(2,1)} %bitcast.12), calls=%async_computation | async-start | bytes 524288 | tf_op jit(solution)/shard_map/near_0/all_to_all | solution.py:156
  31.6 8.6 %all-to-all-done = bf16[4,256,128]{2,1,0:T(8,128)(2,1)S(1)} async-done(((bf16[4,256,128]{2,1,0:T(8,128)(2,1)}), bf16[4,256,128]{2,1,0:T(8,128)(2,1)S(1)}, u32[]{:S(2)}, u32[]{:S(2)}) %all-to-all-start) | async-done | bytes 262176 | tf_op jit(solution)/shard_map/near_0/all_to_all | solution.py:156
  40.3 55.1 %all_to_all.15 = bf16[8,64,128]{2,1,0:T(8,128)(2,1)S(1)} all-to-all(bf16[8,64,128]{2,1,0:T(8,128)(2,1)S(1)} %pad_maximum_fusion), channel_id=1, replica_groups={{0,8,16,24,32,40,48,56},{1,9,17,25,33,41,49,57},{2,10,18,26,34,42,50,58..., dimensions={0} | all-to-all | bytes 262144 | tf_op jit(solution)/shard_map/all_to_all | solution.py:159
  95.4 0.7 reshape.27
  (4 shorter events, 0.1 us)
Async XLA Ops:
  0.0 1.7 %collective-permute-start = (bf16[128,1024]{1,0:T(8,128)(2,1)}, bf16[128,1024]{1,0:T(8,128)(2,1)S(1)}, u32[]{:S(2)}, u32[]{:S(2)}) collective-permute-start(bf16[128,1024]{1,0:T(8,128)(2,1)} %bitcast.16), channel_id=1, source_target_pairs={{0,1},{1,0},{2,3},{3,2},{4,5},{5,4},{6,7},{7,6},{8,9},{9,8},{10,11... | collective-permute-start | bytes 786440 | tf_op jit(solution)/shard_map/ppermute | solution.py:146
  10.8 15.7 %all-to-all-start.1 = ((bf16[4,256,128]{2,1,0:T(8,128)(2,1)}), bf16[4,256,128]{2,1,0:T(8,128)(2,1)S(1)}, u32[]{:S(2)}, u32[]{:S(2)}) async-start(bf16[4,256,128]{2,1,0:T(8,128)(2,1)} %bitcast.13), calls=%async_computation.1 | async-start | bytes 524288 | tf_op jit(solution)/shard_map/near_1/all_to_all | solution.py:156
  26.6 13.6 %all-to-all-start = ((bf16[4,256,128]{2,1,0:T(8,128)(2,1)}), bf16[4,256,128]{2,1,0:T(8,128)(2,1)S(1)}, u32[]{:S(2)}, u32[]{:S(2)}) async-start(bf16[4,256,128]{2,1,0:T(8,128)(2,1)} %bitcast.12), calls=%async_computation | async-start | bytes 524288 | tf_op jit(solution)/shard_map/near_0/all_to_all | solution.py:156

commit v3 on v2

v3 whole, which is shorter than its diff:
```python
import functools
import math

import jax
import jax.numpy as jnp
from jax import lax
from jax.experimental import pallas as pl
from jax.experimental.pallas import tpu as pltpu
from jax.sharding import PartitionSpec as P


CYCLE = 8192
CORES = 2
SHARE = 2
NEAR = 2
TB = 1024
TE = 256
F32 = jnp.float32
BF16 = jnp.bfloat16
SIN = (4.442867903016298, -7.3074434206684415, 3.594788072467163, -0.7843740145897882)
COS = (-1.4142040805466873, 6.977642058572177, -5.7152384030951175, 1.7283486671441728)


def split_cubic(coefs):
    lead = coefs[3]
    a, b = coefs[2] / lead, coefs[1] / lead
    return lead, a, b, coefs[0] / lead - a * b


def centred(value, period):
    return ((value + period // 2) & (period - 1)) - period // 2


def beam_features(chip, core, bin_value, dirs, order, feat, near, share):
    chips = order.shape[0]
    far = chips // (near * share)
    steps = centred(bin_value * dirs[...], CYCLE)
    high = (steps + 32) >> 6
    low = steps - (high << 6)
    shift = (steps[0:1] + steps[1:2] + steps[2:3]) & 31
    terms = [high.astype(F32) * (64.0 / CYCLE), low.astype(F32) * (1.0 / CYCLE), shift.astype(F32) * (256.0 / CYCLE)]
    terms = jnp.concatenate([*terms, jnp.zeros(shift.shape, F32)], axis=0)
    tiles = terms.shape[1] // 128
    table = jnp.concatenate([terms[:, 128 * q : 128 * q + 128] for q in range(tiles)], axis=0).astype(BF16)
    lane = lax.broadcasted_iota(jnp.int32, (1, 128), 1)
    sub = lax.broadcasted_iota(jnp.int32, (128, 128), 0)
    for t in range(near * far // 2):
        rows = []
        for j in (2 * t, 2 * t + 1):
            side = (chip // share + 1 + j // far) % near
            owner = share * (near * (j % far) + side) + chip % share
            rows.append(order[pl.ds(owner, 1), :])
        left = jnp.where(core == 0, rows[0], pltpu.roll(rows[0], 64, 1))
        right = jnp.where(core == 0, pltpu.roll(rows[1], 64, 1), rows[1])
        beam = jnp.where(lane < 64, left, right)
        hot = jnp.where(sub == (beam & 127), 1.0, 0.0).astype(BF16)
        picked = jnp.dot(table, hot, preferred_element_type=F32)
        which = beam >> 7
        total = jnp.zeros((8, 128), F32)
        for q in range(tiles):
            total = jnp.where(which == q, picked[8 * q : 8 * q + 8], total)
        feat[128 * t : 128 * t + 128, :] = total.T.astype(BF16)


def weights_kernel(*refs, near, share, flip, row, tb, te):
    first = flip == 0
    if first:
        bins, mine, other, positions, taper, dirs, order, out, feat, place, turned, pos, tap, sems = refs
    else:
        mine, other, positions, taper, feat, start, out, place, turned, pos, tap, sems = refs
    index = lax.axis_index("blk")
    core = index % CORES
    chip = index // CORES
    source = chip + flip * (1 - 2 * (chip % share))
    count = mine.shape[1]
    copies = []
    for k, owner in enumerate((CORES * source + core, CORES * source + 1 - core)):
        at = pl.ds(pl.multiple_of(owner * count, count), count)
        copies.append(pltpu.make_async_copy(positions.at[:, at], pos.at[k], sems.at[0, k]))
        copies.append(pltpu.make_async_copy(taper.at[:, at], tap.at[k], sems.at[1, k]))
    for copy in copies:
        copy.start()
    if first:
        beam_features(chip, core, bins[0], dirs, order, feat, near, share)
    for copy in copies:
        copy.wait()
    sin_lead, sin_a, sin_b, sin_c = split_cubic(SIN)
    cos_lead, cos_a, cos_b, cos_c = split_cubic(COS)
    ratio = cos_lead / sin_lead
    parts = []
    for k, xs in enumerate((mine, other)):
        where = (pos[k] - 256).astype(F32)
        one = jnp.ones((1, count), F32)
        place[k] = jnp.concatenate([where, where, one, one * 0.0], axis=0).astype(BF16)
        half = xs.shape[0] // 2
        turned[k, :half] = -xs[half:]
        turned[k, half:] = xs[:half]
        amplitude = tap[k] * (1.0 / math.sqrt(taper.shape[1]))
        parts.append((xs, amplitude, amplitude * (sin_lead * sin_lead)))
    contract = (((1,), (1,)), ((), ()))

    def step(i, carry):
        at = pl.multiple_of(i * tb, tb)
        beams = feat[pl.ds(row + at, tb), :]
        total = jnp.zeros((tb, out.shape[1]), F32)
        for k, (xs, amplitude, doubled) in enumerate(parts):
            for e in range(0, count, te):
                cols = slice(e, e + te)
                turns = jnp.dot(beams, place[k, :, cols], preferred_element_type=F32)
                r = turns - jnp.round(turns)
                z = r * r
                w = z * z
                t = r * ((z + sin_a) * (w + sin_b) + sin_c)
                scaled = doubled[:, cols] * t
                weight_re = (amplitude[:, cols] - scaled * t).astype(BF16)
                weight_im = (scaled * ((ratio * z + ratio * cos_a) * (w + cos_b) + ratio * cos_c)).astype(BF16)
                total += lax.dot_general(weight_re, xs[:, cols], contract, preferred_element_type=F32)
                total += lax.dot_general(weight_im, turned[k, :, cols], contract, preferred_element_type=F32)
        if not first:
            total += start[pl.ds(row + at, tb), :]
        out[pl.ds(at, tb), :] = total.astype(out.dtype)
        return carry

    lax.fori_loop(0, out.shape[0] // tb, step, 0)


def partial_beams(flip, operands, near, share, row, beams, kind):
    cols, count = operands[1 - flip].shape
    kernel = functools.partial(weights_kernel, near=near, share=share, flip=flip, row=row, tb=math.gcd(TB, beams), te=TE)
    vmem = pl.BlockSpec(memory_space=pltpu.VMEM)
    hbm = pl.BlockSpec(memory_space=pl.ANY)
    if flip:
        in_specs = [vmem, vmem, hbm, hbm, vmem, vmem]
        out_shape = pltpu.VMEM((beams, cols), kind)
    else:
        in_specs = [pl.BlockSpec(memory_space=pltpu.SMEM), vmem, vmem, hbm, hbm, vmem, vmem]
        out_shape = (pltpu.VMEM((beams, cols), kind), pltpu.VMEM((beams, 8), BF16))
    return pl.pallas_call(
        kernel,
        in_specs=in_specs,
        out_specs=vmem if flip else (vmem, vmem),
        scratch_shapes=[
            pltpu.VMEM((2, 8, count), BF16),
            pltpu.VMEM((2, cols, count), BF16),
            pltpu.VMEM((2, 3, count), jnp.int32),
            pltpu.VMEM((2, 1, count), F32),
            pltpu.SemaphoreType.DMA((2, 2)),
        ],
        out_shape=out_shape,
        cost_estimate=pl.CostEstimate(flops=beams * count * cols * 8, bytes_accessed=2 * cols * count * 4, transcendentals=0),
    )(*operands)


def per_device(snapshots, bin_index, positions, directions, taper, beam_order):
    blocks = lax.axis_size("blk")
    chips = blocks // CORES
    side = SHARE * NEAR
    far = chips // side
    owned = beam_order.shape[0] // blocks
    count = snapshots.shape[1]
    cols = snapshots.shape[2] * snapshots.shape[3]
    beams = beam_order.shape[0] // (CORES * SHARE)

    def swap(value, bit):
        return lax.ppermute(value, "blk", [(i, i ^ bit) for i in range(blocks)])

    def near_by(*values):
        return [pltpu.with_memory_space_constraint(value, pltpu.VMEM) for value in values]

    mine = snapshots[0].transpose(1, 2, 0).reshape(cols, count)
    other = swap(mine, 1)
    across = swap(mine, CORES)
    order = beam_order.reshape(chips, -1)
    (other,) = near_by(other)
    sums, feat = partial_beams(0, (bin_index, mine, other, positions, taper[None], directions, order), NEAR, SHARE, 0, beams, F32)
    across, sums = lax.optimization_barrier((across, sums))
    across_other = swap(across, 1)
    across, across_other, feat, sums = near_by(across, across_other, feat, sums)
    operands = (across, across_other, positions, taper[None], feat, sums)
    half = beams // NEAR
    given = partial_beams(1, operands, NEAR, SHARE, 0, half, BF16)
    given = swap(given, CORES * SHARE)
    kept = partial_beams(1, operands, NEAR, SHARE, half, half, F32)
    sums = (kept + given.astype(F32)).astype(BF16).reshape(far, owned, cols)
    far_groups = [[CORES * (i * side + j) + c for i in range(far)] for j in range(side) for c in range(CORES)]
    sums = lax.all_to_all(sums, "blk", 0, 0, axis_index_groups=far_groups, tiled=True)
    sums = sums.astype(F32).sum(0).astype(BF16)
    return sums.reshape(owned, 1, snapshots.shape[2], snapshots.shape[3])


def solution(mesh):
    return jax.shard_map(
        per_device,
        mesh=mesh,
        in_specs=(P("groups", "blk", None, None), P("groups"), P(), P(), P(), P()),
        out_specs=P("blk", "groups", None, None),
        check_vma=False,
    )
```

time: 96.6 us -> 87.4 us (0.905)
  waiting for transfers between devices: 9.77 us -> 3.46 us
  starting transfers between devices: 11.5 us -> 6.45 us
  blocking collectives: 55.1 us -> 58 us
    all_to_all x2 -> x0, starting transfers between devices: 11.5 us -> none  [per_device(): lax.all_to_all(sums.reshape(NEAR, -1, cols), 'blk', 0, 0, axis_index_grou...]
    all_to_all x2 -> x0, waiting for transfers between devices: 8.68 us -> none  [per_device(): lax.all_to_all(sums.reshape(NEAR, -1, cols), 'blk', 0, 0, axis_index_grou...]
    ppermute x1 -> x4, starting transfers between devices: 0.01 us -> 6.45 us  [swap(): return lax.ppermute(value, 'blk', [(i, i ^ bit) for i in range(blocks)])]
    all_to_all x1, blocking collectives: 55.1 us -> 58 us  [per_device(): lax.all_to_all(sums, 'blk', 0, 0, axis_index_groups=far_groups, tiled=True)]
    ppermute x1 -> x4, waiting for transfers between devices: 1.09 us -> 3.46 us  [swap(): return lax.ppermute(value, 'blk', [(i, i ^ bit) for i in range(blocks)])]
    pallas_call x2 -> x3, Pallas kernels: 18.2 us -> 17.5 us  [partial_beams(): pl.pallas_call(kernel, in_specs=in_specs, out_specs=vmem if flip else (vm...]
  transfers between devices with their start and end apart: 3 -> 4, of which waited for: 3 -> 2; matrix products, arithmetic and copies ran while one was open for 0% -> 0% of each run, Pallas kernels for 9% -> 15%
where the time goes in v3:
time: 87.4 us; the launch traced here: 86.9 us
  blocking collectives  58 us (66%)
  Pallas kernels  17.5 us (20%)
  starting transfers between devices  6.45 us (7%)
  waiting for transfers between devices  3.46 us (4%)
    all_to_all x1, blocking collectives, per_device(): lax.all_to_all(sums, 'blk', 0, 0, axis_index_groups=far_groups, tiled=True)  58 us
    pallas_call x3, Pallas kernels, partial_beams(): pl.pallas_call(kernel, in_specs=in_specs, out_specs=vmem if flip else (vm...  17.5 us
    ppermute x4, starting transfers between devices, swap(): return lax.ppermute(value, 'blk', [(i, i ^ bit) for i in range(blocks)])  6.45 us
    ppermute x4, waiting for transfers between devices, swap(): return lax.ppermute(value, 'blk', [(i, i ^ bit) for i in range(blocks)])  3.46 us
  transfers between devices with their start and end apart: 4, of which 2 were waited for; matrix products, arithmetic and copies ran while one was open for 0% of the time, Pallas kernels for 15%

profile of v3, /device:TPU:38, one launch (start us, length us, event | category | flops | bytes accessed | tf_op | source)
XLA Modules:
  0.0 86.9 jit_solution(12239548274516456097)
XLA Ops:
  0.0 0.0 collective-permute-start.1
  0.0 2.1 %collective-permute-start = (bf16[128,1024]{1,0:T(8,128)(2,1)}, bf16[128,1024]{1,0:T(8,128)(2,1)S(1)}, u32[]{:S(2)}, u32[]{:S(2)}) collective-permute-start(bf16[128,1024]{1,0:T(8,128)(2,1)} %bitcast.13), channel_id=1, source_target_pairs={{0,2},{1,3},{2,0},{3,1},{4,6},{5,7},{6,4},{7,5},{8,10},{9,11},{10,... | collective-permute-start | bytes 786440 | tf_op jit(solution)/shard_map/ppermute | solution.py:165
  2.8 0.0 collective-permute-done.1.refs_2_
  2.8 8.4 %shard_map.64 = (f32[1024,128]{1,0:T(8,128)S(1)}, bf16[1024,8]{1,0:T(8,128)(2,1)S(1)}) custom-call(s32[1]{0:T(128)S(6)} %copy.7.refs_0_, bf16[128,1024]{1,0:T(8,128)(2,1)} %bitcast.14, bf16[128,1024]{1,0:T(8,128)(2,1)S(1)} %collective-permute-done.1.refs_2_, s32[3,65536]{1,0:T(4,128)} %refs_2_.3, f32[1,65536]{1,0:T(1,128)} %bitcast.8, s32[3,4096]{1,0:T(4,128)} %refs_5_.1, ...), custom_call_target="tpu_custom_call" | custom-call | flops 1073741824 | bytes 1048576 | tf_op jit(solution)/shard_map/pallas_call | solution.py:138
  11.2 0.0 collective-permute-done.refs_0_
  11.2 0.5 collective-permute-start.2
  11.7 1.3 %collective-permute-done.2.refs_1_ = bf16[128,1024]{1,0:T(8,128)(2,1)S(1)} collective-permute-done((bf16[128,1024]{1,0:T(8,128)(2,1)S(1)}, bf16[128,1024]{1,0:T(8,128)(2,1)S(1)}, u32[]{:S(2)}, u32[]{:S(2)}) %collective-permute-start.2) | collective-permute-done | bytes 262176 | tf_op jit(solution)/shard_map/ppermute | solution.py:165
  13.1 4.6 %shard_map.66 = bf16[512,128]{1,0:T(8,128)(2,1)S(1)} custom-call(bf16[128,1024]{1,0:T(8,128)(2,1)S(1)} %collective-permute-done.refs_0_, bf16[128,1024]{1,0:T(8,128)(2,1)S(1)} %collective-permute-done.2.refs_1_, s32[3,65536]{1,0:T(4,128)} %refs_2_.3, f32[1,65536]{1,0:T(1,128)} %bitcast.9, bf16[1024,8]{1,0:T(8,128)(2,1)S(1)} %get-tuple-element.11.refs_4_, ...), custom_call_target="tpu_custom_call" | custom-call | flops 536870912 | bytes 1048576 | tf_op jit(solution)/shard_map/pallas_call | solution.py:138
  17.6 3.8 %collective-permute-start.3 = (bf16[512,128]{1,0:T(8,128)(2,1)S(1)}, bf16[512,128]{1,0:T(8,128)(2,1)S(1)}, u32[]{:S(2)}, u32[]{:S(2)}) collective-permute-start(bf16[512,128]{1,0:T(8,128)(2,1)S(1)} %shard_map.66), channel_id=1, source_target_pairs={{0,4},{1,5},{2,6},{3,7},{4,0},{5,1},{6,2},{7,3},{8,12},{9,13},{10,... | collective-permute-start | bytes 393224 | tf_op jit(solution)/shard_map/ppermute | solution.py:165
  21.4 4.6 %shard_map.65 = f32[512,128]{1,0:T(8,128)S(1)} custom-call(bf16[128,1024]{1,0:T(8,128)(2,1)S(1)} %collective-permute-done.refs_0_, bf16[128,1024]{1,0:T(8,128)(2,1)S(1)} %collective-permute-done.2.refs_1_, s32[3,65536]{1,0:T(4,128)} %refs_2_.3, f32[1,65536]{1,0:T(1,128)} %bitcast.10, bf16[1024,8]{1,0:T(8,128)(2,1)S(1)} %get-tuple-element.11.refs_4_, ...), custom_call_target="tpu_custom_call" | custom-call | flops 536870912 | bytes 1048576 | tf_op jit(solution)/shard_map/pallas_call | solution.py:138
  26.0 2.1 %collective-permute-done.3 = bf16[512,128]{1,0:T(8,128)(2,1)S(1)} collective-permute-done((bf16[512,128]{1,0:T(8,128)(2,1)S(1)}, bf16[512,128]{1,0:T(8,128)(2,1)S(1)}, u32[]{:S(2)}, u32[]{:S(2)}) %collective-permute-start.3) | collective-permute-done | bytes 131104 | tf_op jit(solution)/shard_map/ppermute | solution.py:165
  28.2 58.0 %all_to_all.5 = bf16[8,64,128]{2,1,0:T(8,128)(2,1)S(1)} all-to-all(bf16[8,64,128]{2,1,0:T(8,128)(2,1)S(1)} %bitcast.11), channel_id=1, replica_groups={{0,8,16,24,32,40,48,56},{1,9,17,25,33,41,49,57},{2,10,18,26,34,42,50,58..., dimensions={0} | all-to-all | bytes 262144 | tf_op jit(solution)/shard_map/all_to_all | solution.py:186
  86.2 0.7 reshape.15
  (2 shorter events, 0.1 us)
Async XLA Ops:
  0.0 2.8 %collective-permute-start.1 = (bf16[128,1024]{1,0:T(8,128)(2,1)}, bf16[128,1024]{1,0:T(8,128)(2,1)S(1)}, u32[]{:S(2)}, u32[]{:S(2)}) collective-permute-start(bf16[128,1024]{1,0:T(8,128)(2,1)} %bitcast.12), channel_id=1, source_target_pairs={{0,1},{1,0},{2,3},{3,2},{4,5},{5,4},{6,7},{7,6},{8,9},{9,8},{10,11... | collective-permute-start | bytes 786440 | tf_op jit(solution)/shard_map/ppermute | solution.py:165
  0.0 11.2 %collective-permute-start = (bf16[128,1024]{1,0:T(8,128)(2,1)}, bf16[128,1024]{1,0:T(8,128)(2,1)S(1)}, u32[]{:S(2)}, u32[]{:S(2)}) collective-permute-start(bf16[128,1024]{1,0:T(8,128)(2,1)} %bitcast.13), channel_id=1, source_target_pairs={{0,2},{1,3},{2,0},{3,1},{4,6},{5,7},{6,4},{7,5},{8,10},{9,11},{10,... | collective-permute-start | bytes 786440 | tf_op jit(solution)/shard_map/ppermute | solution.py:165
  11.2 1.8 %collective-permute-start.2 = (bf16[128,1024]{1,0:T(8,128)(2,1)S(1)}, bf16[128,1024]{1,0:T(8,128)(2,1)S(1)}, u32[]{:S(2)}, u32[]{:S(2)}) collective-permute-start(bf16[128,1024]{1,0:T(8,128)(2,1)S(1)} %collective-permute-done.refs_0_), channel_id=1, source_target_pairs={{0,1},{1,0},{2,3},{3,2},{4,5},{5,4},{6,7},{7,6},{8,9},{9,8},{10,11... | collective-permute-start | bytes 786440 | tf_op jit(solution)/shard_map/ppermute | solution.py:165
  17.6 10.5 %collective-permute-start.3 = (bf16[512,128]{1,0:T(8,128)(2,1)S(1)}, bf16[512,128]{1,0:T(8,128)(2,1)S(1)}, u32[]{:S(2)}, u32[]{:S(2)}) collective-permute-start(bf16[512,128]{1,0:T(8,128)(2,1)S(1)} %shard_map.66), channel_id=1, source_target_pairs={{0,4},{1,5},{2,6},{3,7},{4,0},{5,1},{6,2},{7,3},{8,12},{9,13},{10,... | collective-permute-start | bytes 393224 | tf_op jit(solution)/shard_map/ppermute | solution.py:165

commit v4 on v3

v4 whole, which is shorter than its diff:
```python
import functools
import math

import jax
import jax.numpy as jnp
from jax import lax
from jax.experimental import pallas as pl
from jax.experimental.pallas import tpu as pltpu
from jax.sharding import PartitionSpec as P


CYCLE = 8192
CORES = 2
SHARE = 2
TB = 512
TE = 256
F32 = jnp.float32
BF16 = jnp.bfloat16
SIN = (4.442867903016298, -7.3074434206684415, 3.594788072467163, -0.7843740145897882)
COS = (-1.4142040805466873, 6.977642058572177, -5.7152384030951175, 1.7283486671441728)


def split_cubic(coefs):
    lead = coefs[3]
    a, b = coefs[2] / lead, coefs[1] / lead
    return lead, a, b, coefs[0] / lead - a * b


def centred(value, period):
    return ((value + period // 2) & (period - 1)) - period // 2


def owner_of(j, chip, chips, share):
    side = 2 * share
    far = chips // side
    near = (chip ^ share) if j < far else chip
    return side * (j % far) + near % side


def beam_features(chip, core, bin_value, dirs, order, feat, share):
    chips = order.shape[0]
    steps = centred(bin_value * dirs[...], CYCLE)
    high = (steps + 32) >> 6
    low = steps - (high << 6)
    shift = (steps[0:1] + steps[1:2] + steps[2:3]) & 31
    terms = [high.astype(F32) * (64.0 / CYCLE), low.astype(F32) * (1.0 / CYCLE), shift.astype(F32) * (256.0 / CYCLE)]
    terms = jnp.concatenate([*terms, jnp.zeros(shift.shape, F32)], axis=0)
    tiles = terms.shape[1] // 128
    table = jnp.concatenate([terms[:, 128 * q : 128 * q + 128] for q in range(tiles)], axis=0).astype(BF16)
    lane = lax.broadcasted_iota(jnp.int32, (1, 128), 1)
    sub = lax.broadcasted_iota(jnp.int32, (128, 128), 0)
    for t in range(chips // share // 2):
        rows = []
        for j in (2 * t, 2 * t + 1):
            owner = owner_of(j, chip, chips, share)
            rows.append(order[pl.ds(owner, 1), :])
        left = jnp.where(core == 0, rows[0], pltpu.roll(rows[0], 64, 1))
        right = jnp.where(core == 0, pltpu.roll(rows[1], 64, 1), rows[1])
        beam = jnp.where(lane < 64, left, right)
        hot = jnp.where(sub == (beam & 127), 1.0, 0.0).astype(BF16)
        picked = jnp.dot(table, hot, preferred_element_type=F32)
        which = beam >> 7
        total = jnp.zeros((8, 128), F32)
        for q in range(tiles):
            total = jnp.where(which == q, picked[8 * q : 8 * q + 8], total)
        feat[128 * t : 128 * t + 128, :] = total.T.astype(BF16)


def element_features(index, positions, taper, place, shade, pos, sems):
    parts, _, count = pos.shape
    copies = []
    for k in range(parts):
        at = pl.ds(pl.multiple_of((index ^ k) * count, count), count)
        copies.append(pltpu.make_async_copy(positions.at[:, at], pos.at[k], sems.at[0, k]))
        copies.append(pltpu.make_async_copy(taper.at[:, at], shade.at[k], sems.at[1, k]))
    for copy in copies:
        copy.start()
    yield
    for copy in copies:
        copy.wait()
    one = jnp.ones((1, count), F32)
    for k in range(parts):
        where = (pos[k] - 256).astype(F32)
        place[k] = jnp.concatenate([where, where, one, one * 0.0], axis=0).astype(BF16)
        shade[k] = shade[k] * (1.0 / math.sqrt(taper.shape[1]))


def weigh(xs_refs, pieces, feat, place, shade, turned, start, out, row, tb, te):
    count = place.shape[2]
    sin_lead, sin_a, sin_b, sin_c = split_cubic(SIN)
    cos_lead, cos_a, cos_b, cos_c = split_cubic(COS)
    ratio = cos_lead / sin_lead
    parts = []
    for slot, (xs, k) in enumerate(zip(xs_refs, pieces)):
        half = xs.shape[0] // 2
        turned[slot, :half] = -xs[half:]
        turned[slot, half:] = xs[:half]
        amplitude = shade[k]
        parts.append((xs, k, slot, amplitude, amplitude * (sin_lead * sin_lead)))
    contract = (((1,), (1,)), ((), ()))

    def step(i, carry):
        at = pl.multiple_of(i * tb, tb)
        beams = feat[pl.ds(row + at, tb), :]
        total = jnp.zeros((tb, out.shape[1]), F32) if start is None else start[pl.ds(at, tb), :]
        for xs, k, slot, amplitude, doubled in parts:
            for e in range(0, count, te):
                cols = slice(e, e + te)
                turns = jnp.dot(beams, place[k, :, cols], preferred_element_type=F32)
                r = turns - jnp.round(turns)
                z = r * r
                w = z * z
                t = r * ((z + sin_a) * (w + sin_b) + sin_c)
                scaled = doubled[:, cols] * t
                weight_re = (amplitude[:, cols] - scaled * t).astype(BF16)
                weight_im = (scaled * ((ratio * z + ratio * cos_a) * (w + cos_b) + ratio * cos_c)).astype(BF16)
                total += lax.dot_general(weight_re, xs[:, cols], contract, preferred_element_type=F32)
                total += lax.dot_general(weight_im, turned[slot, :, cols], contract, preferred_element_type=F32)
        out[pl.ds(at, tb), :] = total.astype(out.dtype)
        return carry

    lax.fori_loop(0, out.shape[0] // tb, step, 0)


def first_kernel(bins, mine, other, positions, taper, dirs, order, out, feat, place, shade, turned, pos, sems, *, share, tb, te):
    index = lax.axis_index("blk")
    elements = element_features(index, positions, taper, place, shade, pos, sems)
    next(elements)
    beam_features(index // CORES, index % CORES, bins[0], dirs, order, feat, share)
    next(elements, None)
    weigh((mine, other), (0, 1), feat, place, shade, turned, None, out, 0, tb, te)


def given_kernel(xs, feat, place, shade, start, out, turned, *, piece, tb, te):
    weigh((xs,), (piece,), feat, place, shade, turned, start, out, 0, tb, te)


def kept_kernel(mine, other, across, across_other, feat, place, shade, out, turned, *, row, tb, te):
    weigh((mine, other, across, across_other), (0, 1, 2, 3), feat, place, shade, turned, None, out, row, tb, te)


def per_device(snapshots, bin_index, positions, directions, taper, beam_order):
    blocks = lax.axis_size("blk")
    chips = blocks // CORES
    parts = CORES * SHARE
    count = snapshots.shape[1]
    cols = snapshots.shape[2] * snapshots.shape[3]
    beams = beam_order.shape[0] // parts
    half = beams // 2
    vmem = pl.BlockSpec(memory_space=pltpu.VMEM)
    hbm = pl.BlockSpec(memory_space=pl.ANY)

    def swap(value, bit):
        return lax.ppermute(value, "blk", [(i, i ^ bit) for i in range(blocks)])

    def near_by(*values):
        return [pltpu.with_memory_space_constraint(value, pltpu.VMEM) for value in values]

    def call(kernel, in_specs, out_shape, scratch, operands, slots):
        return pl.pallas_call(
            kernel,
            in_specs=in_specs,
            out_specs=jax.tree.map(lambda _: vmem, out_shape),
            out_shape=out_shape,
            scratch_shapes=[pltpu.VMEM((slots, cols, count), BF16), *scratch],
            cost_estimate=pl.CostEstimate(flops=half * slots * count * cols * 8, bytes_accessed=2 * cols * count * 4, transcendentals=0),
        )(*operands)

    mine = snapshots[0].transpose(1, 2, 0).reshape(cols, count)
    other = swap(mine, 1)
    across = swap(mine, CORES)
    order = beam_order.reshape(chips, -1)
    (other,) = near_by(other)
    sums, feat, place, shade = call(
        functools.partial(first_kernel, share=SHARE, tb=math.gcd(TB, half), te=TE),
        [pl.BlockSpec(memory_space=pltpu.SMEM), vmem, vmem, hbm, hbm, vmem, vmem],
        (
            pltpu.VMEM((half, cols), F32),
            pltpu.VMEM((beams, 8), BF16),
            pltpu.VMEM((parts, 8, count), BF16),
            pltpu.VMEM((parts, 1, count), F32),
        ),
        [pltpu.VMEM((parts, 3, count), jnp.int32), pltpu.SemaphoreType.DMA((2, parts))],
        (bin_index, mine, other, positions, taper[None], directions, order),
        2,
    )
    across, sums = lax.optimization_barrier((across, sums))
    across_other = swap(across, 1)
    across, across_other, feat, place, shade, sums = near_by(across, across_other, feat, place, shade, sums)

    def give(xs, piece, start, kind):
        return call(
            functools.partial(given_kernel, piece=piece, tb=math.gcd(TB, half), te=TE),
            [vmem] * 5,
            pltpu.VMEM((half, cols), kind),
            [],
            (xs, feat, place, shade, start),
            1,
        )

    (sums,) = near_by(give(across, 2, sums, F32))
    given = give(across_other, 3, sums, BF16)
    given = swap(given, CORES * SHARE)
    kept = call(
        functools.partial(kept_kernel, row=half, tb=math.gcd(TB, half), te=TE),
        [vmem] * 7,
        pltpu.VMEM((half, cols), F32),
        [],
        (*near_by(mine), other, across, across_other, feat, place, shade),
        4,
    )
    sums = kept + given.astype(F32)
    side = SHARE * 2
    far = chips // side
    far_groups = [[CORES * (i * side + j) + c for i in range(far)] for j in range(side) for c in range(CORES)]
    sums = sums.astype(BF16).reshape(far, -1, cols)
    sums = lax.all_to_all(sums, "blk", 0, 0, axis_index_groups=far_groups, tiled=True)
    sums = sums.astype(F32).sum(0).astype(BF16)
    return sums.reshape(-1, 1, snapshots.shape[2], snapshots.shape[3])


def solution(mesh):
    return jax.shard_map(
        per_device,
        mesh=mesh,
        in_specs=(P("groups", "blk", None, None), P("groups"), P(), P(), P(), P()),
        out_specs=P("blk", "groups", None, None),
        check_vma=False,
    )
```

time: 87.4 us -> 84 us (0.961)
  Pallas kernels: 17.5 us -> 15.6 us
  waiting for transfers between devices: 3.46 us -> 1.6 us
  blocking collectives: 58 us -> 58.9 us
    pallas_call x3 -> x4, Pallas kernels: 17.5 us -> 15.6 us  [call(): pl.pallas_call(kernel, in_specs=in_specs, out_specs=jax.tree.map(lambda _...]
    ppermute x4, waiting for transfers between devices: 3.46 us -> 1.6 us  [swap(): return lax.ppermute(value, 'blk', [(i, i ^ bit) for i in range(blocks)])]
    all_to_all x1, blocking collectives: 58 us -> 58.9 us  [per_device(): lax.all_to_all(sums, 'blk', 0, 0, axis_index_groups=far_groups, tiled=True)]
  transfers between devices with their start and end apart: 4 -> 4, of which waited for: 2 -> 2; matrix products, arithmetic and copies ran while one was open for 0% -> 0% of each run, Pallas kernels for 15% -> 16%
where the time goes in v4:
time: 84 us; the launch traced here: 83.7 us
  blocking collectives  58.9 us (70%)
  Pallas kernels  15.6 us (19%)
  starting transfers between devices  6.09 us (7%)
  waiting for transfers between devices  1.6 us (2%)
    all_to_all x1, blocking collectives, per_device(): lax.all_to_all(sums, 'blk', 0, 0, axis_index_groups=far_groups, tiled=True)  58.9 us
    pallas_call x4, Pallas kernels, call(): pl.pallas_call(kernel, in_specs=in_specs, out_specs=jax.tree.map(lambda _...  15.6 us
    ppermute x4, starting transfers between devices, swap(): return lax.ppermute(value, 'blk', [(i, i ^ bit) for i in range(blocks)])  6.09 us
  transfers between devices with their start and end apart: 4, of which 2 were waited for; matrix products, arithmetic and copies ran while one was open for 0% of the time, Pallas kernels for 16%

profile of v4, /device:TPU:38, one launch (start us, length us, event | category | flops | bytes accessed | tf_op | source)
XLA Modules:
  0.0 83.7 jit_solution(9893636596793170881)
XLA Ops:
  0.0 0.0 collective-permute-start
  0.0 2.1 %collective-permute-start.1 = (bf16[128,1024]{1,0:T(8,128)(2,1)}, bf16[128,1024]{1,0:T(8,128)(2,1)S(1)}, u32[]{:S(2)}, u32[]{:S(2)}) collective-permute-start(bf16[128,1024]{1,0:T(8,128)(2,1)} %bitcast.9), channel_id=1, source_target_pairs={{0,2},{1,3},{2,0},{3,1},{4,6},{5,7},{6,4},{7,5},{8,10},{9,11},{10,... | collective-permute-start | bytes 786440 | tf_op jit(solution)/shard_map/ppermute | solution.py:154
  2.8 0.0 collective-permute-done.other
  2.8 5.4 %shard_map.64 = (f32[512,128]{1,0:T(8,128)S(1)}, bf16[1024,8]{1,0:T(8,128)(2,1)S(1)}, bf16[4,8,1024]{2,1,0:T(8,128)(2,1)S(1)}, f32[4,1,1024]{2,1,0:T(1,128)S(1)}) custom-call(s32[1]{0:T(128)S(6)} %copy.7.bins, bf16[128,1024]{1,0:T(8,128)(2,1)} %bitcast.10, bf16[128,1024]{1,0:T(8,128)(2,1)S(1)} %collective-permute-done.other, s32[3,65536]{1,0:T(4,128)} %positions.1, ...), custom_call_target="tpu_custom_call" | custom-call | flops 1073741824 | bytes 1048576 | tf_op jit(solution)/shard_map/pallas_call | solution.py:160
  8.2 1.1 %collective-permute-done.1.across.xs = bf16[128,1024]{1,0:T(8,128)(2,1)S(1)} collective-permute-done((bf16[128,1024]{1,0:T(8,128)(2,1)}, bf16[128,1024]{1,0:T(8,128)(2,1)S(1)}, u32[]{:S(2)}, u32[]{:S(2)}) %collective-permute-start.1) | collective-permute-done | bytes 262176 | tf_op jit(solution)/shard_map/ppermute | solution.py:154
  9.3 0.0 collective-permute-start.2
  9.3 1.9 %shard_map.66.start = f32[512,128]{1,0:T(8,128)S(1)} custom-call(bf16[128,1024]{1,0:T(8,128)(2,1)S(1)} %collective-permute-done.1.across.xs, bf16[1024,8]{1,0:T(8,128)(2,1)S(1)} %get-tuple-element.13.feat, bf16[4,8,1024]{2,1,0:T(8,128)(2,1)S(1)} %get-tuple-element.14.place, f32[4,1,1024]{2,1,0:T(1,128)S(1)} %get-tuple-element.15.shade, ...), custom_call_target="tpu_custom_call" | custom-call | flops 536870912 | bytes 1048576 | tf_op jit(solution)/shard_map/pallas_call | solution.py:160
  11.2 0.0 copy-start
  11.2 0.0 collective-permute-done.2.across_other.xs
  11.2 1.9 %shard_map.67 = bf16[512,128]{1,0:T(8,128)(2,1)S(1)} custom-call(bf16[128,1024]{1,0:T(8,128)(2,1)S(1)} %collective-permute-done.2.across_other.xs, bf16[1024,8]{1,0:T(8,128)(2,1)S(1)} %get-tuple-element.13.feat, bf16[4,8,1024]{2,1,0:T(8,128)(2,1)S(1)} %get-tuple-element.14.place, f32[4,1,1024]{2,1,0:T(1,128)S(1)} %get-tuple-element.15.shade, ...), custom_call_target="tpu_custom_call" | custom-call | flops 536870912 | bytes 1048576 | tf_op jit(solution)/shard_map/pallas_call | solution.py:160
  13.1 4.0 %collective-permute-start.3 = (bf16[512,128]{1,0:T(8,128)(2,1)S(1)}, bf16[512,128]{1,0:T(8,128)(2,1)S(1)}, u32[]{:S(2)}, u32[]{:S(2)}) collective-permute-start(bf16[512,128]{1,0:T(8,128)(2,1)S(1)} %shard_map.67), channel_id=1, source_target_pairs={{0,4},{1,5},{2,6},{3,7},{4,0},{5,1},{6,2},{7,3},{8,12},{9,13},{10,... | collective-permute-start | bytes 393224 | tf_op jit(solution)/shard_map/ppermute | solution.py:154
  17.0 0.0 copy-done
  17.0 6.5 %shard_map.65 = f32[512,128]{1,0:T(8,128)S(1)} custom-call(bf16[128,1024]{1,0:T(8,128)(2,1)S(1)} %bitcast.11, bf16[128,1024]{1,0:T(8,128)(2,1)S(1)} %collective-permute-done.other, bf16[128,1024]{1,0:T(8,128)(2,1)S(1)} %collective-permute-done.1.across.xs, bf16[128,1024]{1,0:T(8,128)(2,1)S(1)} %collective-permute-done.2.across_other.xs, ...), custom_call_target="tpu_custom_call" | custom-call | flops 2147483648 | bytes 1048576 | tf_op jit(solution)/shard_map/pallas_call | solution.py:160
  23.6 0.5 collective-permute-done.3
  24.1 58.9 %all_to_all.5 = bf16[8,64,128]{2,1,0:T(8,128)(2,1)S(1)} all-to-all(bf16[8,64,128]{2,1,0:T(8,128)(2,1)S(1)} %bitcast.12), channel_id=1, replica_groups={{0,8,16,24,32,40,48,56},{1,9,17,25,33,41,49,57},{2,10,18,26,34,42,50,58..., dimensions={0} | all-to-all | bytes 262144 | tf_op jit(solution)/shard_map/all_to_all | solution.py:217
  83.0 0.7 reshape.15
  (2 shorter events, 0.1 us)
Async XLA Ops:
  0.0 2.8 %collective-permute-start = (bf16[128,1024]{1,0:T(8,128)(2,1)}, bf16[128,1024]{1,0:T(8,128)(2,1)S(1)}, u32[]{:S(2)}, u32[]{:S(2)}) collective-permute-start(bf16[128,1024]{1,0:T(8,128)(2,1)} %bitcast.8), channel_id=1, source_target_pairs={{0,1},{1,0},{2,3},{3,2},{4,5},{5,4},{6,7},{7,6},{8,9},{9,8},{10,11... | collective-permute-start | bytes 786440 | tf_op jit(solution)/shard_map/ppermute | solution.py:154
  0.0 9.3 %collective-permute-start.1 = (bf16[128,1024]{1,0:T(8,128)(2,1)}, bf16[128,1024]{1,0:T(8,128)(2,1)S(1)}, u32[]{:S(2)}, u32[]{:S(2)}) collective-permute-start(bf16[128,1024]{1,0:T(8,128)(2,1)} %bitcast.9), channel_id=1, source_target_pairs={{0,2},{1,3},{2,0},{3,1},{4,6},{5,7},{6,4},{7,5},{8,10},{9,11},{10,... | collective-permute-start | bytes 786440 | tf_op jit(solution)/shard_map/ppermute | solution.py:154
  9.3 1.9 %collective-permute-start.2 = (bf16[128,1024]{1,0:T(8,128)(2,1)S(1)}, bf16[128,1024]{1,0:T(8,128)(2,1)S(1)}, u32[]{:S(2)}, u32[]{:S(2)}) collective-permute-start(bf16[128,1024]{1,0:T(8,128)(2,1)S(1)} %collective-permute-done.1.across.xs), channel_id=1, source_target_pairs={{0,1},{1,0},{2,3},{3,2},{4,5},{5,4},{6,7},{7,6},{8,9},{9,8},{10,11... | collective-permute-start | bytes 786440 | tf_op jit(solution)/shard_map/ppermute | solution.py:154
  11.2 5.9 %copy-start = (bf16[1,1024,2,64]{1,3,2,0:T(8,128)(2,1)S(1)}, bf16[1,1024,2,64]{1,3,2,0:T(8,128)(2,1)}, u32[]{:S(2)}) copy-start(bf16[1,1024,2,64]{1,3,2,0:T(8,128)(2,1)} %param.6) | copy-start | bytes 786436
  13.1 11.0 %collective-permute-start.3 = (bf16[512,128]{1,0:T(8,128)(2,1)S(1)}, bf16[512,128]{1,0:T(8,128)(2,1)S(1)}, u32[]{:S(2)}, u32[]{:S(2)}) collective-permute-start(bf16[512,128]{1,0:T(8,128)(2,1)S(1)} %shard_map.67), channel_id=1, source_target_pairs={{0,4},{1,5},{2,6},{3,7},{4,0},{5,1},{6,2},{7,3},{8,12},{9,13},{10,... | collective-permute-start | bytes 393224 | tf_op jit(solution)/shard_map/ppermute | solution.py:154

commit v5 on v4

--- a/solution.py
+++ b/solution.py
@@ -12,6 +12,7 @@
 CYCLE = 8192
 CORES = 2
 SHARE = 2
+HOPS = (-2, 1, 4, -1, 2, -3, 0, 3)
 TB = 512
 TE = 256
 F32 = jnp.float32
@@ -34,7 +35,7 @@
     side = 2 * share
     far = chips // side
     near = (chip ^ share) if j < far else chip
-    return side * (j % far) + near % side
+    return side * ((chip // side + HOPS[j % far]) % far) + near % side
 
 
 def beam_features(chip, core, bin_value, dirs, order, feat, share):
@@ -210,13 +211,18 @@
         4,
     )
     sums = kept + given.astype(F32)
-    side = SHARE * 2
-    far = chips // side
-    far_groups = [[CORES * (i * side + j) + c for i in range(far)] for j in range(side) for c in range(CORES)]
-    sums = sums.astype(BF16).reshape(far, -1, cols)
-    sums = lax.all_to_all(sums, "blk", 0, 0, axis_index_groups=far_groups, tiled=True)
-    sums = sums.astype(F32).sum(0).astype(BF16)
-    return sums.reshape(-1, 1, snapshots.shape[2], snapshots.shape[3])
+    side = CORES * SHARE * 2
+    rows = half // len(HOPS)
+
+    def shift(value, far):
+        return lax.ppermute(value.astype(BF16), "blk", [(i, (i + far * side) % blocks) for i in range(blocks)]).astype(F32)
+
+    up = shift(sums[: 3 * rows], 1)
+    down = shift(sums[3 * rows : 5 * rows], -1)
+    sums = sums[5 * rows :] + up
+    below, own, above = sums[:rows], sums[rows : 2 * rows] + down[:rows], sums[2 * rows :] + down[rows:]
+    sums = own + shift(above, 3) + shift(below, -3)
+    return sums.astype(BF16).reshape(-1, 1, snapshots.shape[2], snapshots.shape[3])
 
 
 def solution(mesh):

time: 84 us -> 80 us (0.952)
  blocking collectives: 58.9 us -> 0 us
  starting transfers between devices: 6.09 us -> 44.3 us
  waiting for transfers between devices: 1.6 us -> 18.2 us
    all_to_all x1 -> x0, blocking collectives: 58.9 us -> none  [per_device(): lax.all_to_all(sums, 'blk', 0, 0, axis_index_groups=far_groups, tiled=True)]
    ppermute x0 -> x4, starting transfers between devices: none -> 38.3 us  [shift(): lax.ppermute(value.astype(BF16), 'blk', [(i, (i + far * side) % blocks) f...]
    ppermute x0 -> x4, waiting for transfers between devices: none -> 16.7 us  [shift(): lax.ppermute(value.astype(BF16), 'blk', [(i, (i + far * side) % blocks) f...]
  transfers between devices with their start and end apart: 4 -> 8, of which waited for: 2 -> 6; matrix products, arithmetic and copies ran while one was open for 0% -> 0% of each run, Pallas kernels for 16% -> 17%
where the time goes in v5:
time: 80 us; the launch traced here: 79.8 us
  starting transfers between devices  44.3 us (55%)
  waiting for transfers between devices  18.2 us (23%)
  Pallas kernels  15.7 us (20%)
    ppermute x4, starting transfers between devices, shift(): lax.ppermute(value.astype(BF16), 'blk', [(i, (i + far * side) % blocks) f...  38.3 us
    ppermute x4, waiting for transfers between devices, shift(): lax.ppermute(value.astype(BF16), 'blk', [(i, (i + far * side) % blocks) f...  16.7 us
    pallas_call x4, Pallas kernels, call(): pl.pallas_call(kernel, in_specs=in_specs, out_specs=jax.tree.map(lambda _...  15.7 us
    ppermute x4, starting transfers between devices, swap(): return lax.ppermute(value, 'blk', [(i, i ^ bit) for i in range(blocks)])  6.09 us
  transfers between devices with their start and end apart: 8, of which 6 were waited for; matrix products, arithmetic and copies ran while one was open for 0% of the time, Pallas kernels for 17%

profile of v5, /device:TPU:38, one launch (start us, length us, event | category | flops | bytes accessed | tf_op | source)
XLA Modules:
  0.0 79.8 jit_solution(17066864541226017526)
XLA Ops:
  0.0 0.0 collective-permute-start
  0.0 2.1 %collective-permute-start.1 = (bf16[128,1024]{1,0:T(8,128)(2,1)}, bf16[128,1024]{1,0:T(8,128)(2,1)S(1)}, u32[]{:S(2)}, u32[]{:S(2)}) collective-permute-start(bf16[128,1024]{1,0:T(8,128)(2,1)} %bitcast.9), channel_id=1, source_target_pairs={{0,2},{1,3},{2,0},{3,1},{4,6},{5,7},{6,4},{7,5},{8,10},{9,11},{10,... | collective-permute-start | bytes 786440 | tf_op jit(solution)/shard_map/ppermute | solution.py:155
  2.8 0.0 collective-permute-done.other
  2.8 5.5 %shard_map.64 = (f32[512,128]{1,0:T(8,128)S(1)}, bf16[1024,8]{1,0:T(8,128)(2,1)S(1)}, bf16[4,8,1024]{2,1,0:T(8,128)(2,1)S(1)}, f32[4,1,1024]{2,1,0:T(1,128)S(1)}) custom-call(s32[1]{0:T(128)S(6)} %copy.8.bins, bf16[128,1024]{1,0:T(8,128)(2,1)} %bitcast.10, bf16[128,1024]{1,0:T(8,128)(2,1)S(1)} %collective-permute-done.other, s32[3,65536]{1,0:T(4,128)} %positions.1, ...), custom_call_target="tpu_custom_call" | custom-call | flops 1073741824 | bytes 1048576 | tf_op jit(solution)/shard_map/pallas_call | solution.py:161
  8.3 1.0 %collective-permute-done.1.across.xs = bf16[128,1024]{1,0:T(8,128)(2,1)S(1)} collective-permute-done((bf16[128,1024]{1,0:T(8,128)(2,1)}, bf16[128,1024]{1,0:T(8,128)(2,1)S(1)}, u32[]{:S(2)}, u32[]{:S(2)}) %collective-permute-start.1) | collective-permute-done | bytes 262176 | tf_op jit(solution)/shard_map/ppermute | solution.py:155
  9.3 0.0 collective-permute-start.2
  9.3 1.9 %shard_map.66.start = f32[512,128]{1,0:T(8,128)S(1)} custom-call(bf16[128,1024]{1,0:T(8,128)(2,1)S(1)} %collective-permute-done.1.across.xs, bf16[1024,8]{1,0:T(8,128)(2,1)S(1)} %get-tuple-element.13.feat, bf16[4,8,1024]{2,1,0:T(8,128)(2,1)S(1)} %get-tuple-element.14.place, f32[4,1,1024]{2,1,0:T(1,128)S(1)} %get-tuple-element.15.shade, ...), custom_call_target="tpu_custom_call" | custom-call | flops 536870912 | bytes 1048576 | tf_op jit(solution)/shard_map/pallas_call | solution.py:161
  11.2 0.0 copy-start
  11.2 0.0 collective-permute-done.2.across_other.xs
  11.2 1.9 %shard_map.67 = bf16[512,128]{1,0:T(8,128)(2,1)S(1)} custom-call(bf16[128,1024]{1,0:T(8,128)(2,1)S(1)} %collective-permute-done.2.across_other.xs, bf16[1024,8]{1,0:T(8,128)(2,1)S(1)} %get-tuple-element.13.feat, bf16[4,8,1024]{2,1,0:T(8,128)(2,1)S(1)} %get-tuple-element.14.place, f32[4,1,1024]{2,1,0:T(1,128)S(1)} %get-tuple-element.15.shade, ...), custom_call_target="tpu_custom_call" | custom-call | flops 536870912 | bytes 1048576 | tf_op jit(solution)/shard_map/pallas_call | solution.py:161
  13.1 4.0 %collective-permute-start.3 = (bf16[512,128]{1,0:T(8,128)(2,1)S(1)}, bf16[512,128]{1,0:T(8,128)(2,1)S(1)}, u32[]{:S(2)}, u32[]{:S(2)}) collective-permute-start(bf16[512,128]{1,0:T(8,128)(2,1)S(1)} %shard_map.67), channel_id=1, source_target_pairs={{0,4},{1,5},{2,6},{3,7},{4,0},{5,1},{6,2},{7,3},{8,12},{9,13},{10,... | collective-permute-start | bytes 393224 | tf_op jit(solution)/shard_map/ppermute | solution.py:155
  17.0 0.0 copy-done
  17.0 6.5 %shard_map.65 = f32[512,128]{1,0:T(8,128)S(1)} custom-call(bf16[128,1024]{1,0:T(8,128)(2,1)S(1)} %bitcast.11, bf16[128,1024]{1,0:T(8,128)(2,1)S(1)} %collective-permute-done.other, bf16[128,1024]{1,0:T(8,128)(2,1)S(1)} %collective-permute-done.1.across.xs, bf16[128,1024]{1,0:T(8,128)(2,1)S(1)} %collective-permute-done.2.across_other.xs, ...), custom_call_target="tpu_custom_call" | custom-call | flops 2147483648 | bytes 1048576 | tf_op jit(solution)/shard_map/pallas_call | solution.py:161
  23.6 0.5 collective-permute-done.3
  24.1 8.1 %collective-permute-start.4 = (bf16[192,128]{1,0:T(8,128)(2,1)S(1)}, bf16[192,128]{1,0:T(8,128)(2,1)S(1)}, u32[]{:S(2)}, u32[]{:S(2)}) collective-permute-start(bf16[192,128]{1,0:T(8,128)(2,1)S(1)} %slice.36), channel_id=1, source_target_pairs={{0,8},{1,9},{2,10},{3,11},{4,12},{5,13},{6,14},{7,15},{8,16},{9,17... | collective-permute-start | bytes 147464 | tf_op jit(solution)/shard_map/ppermute | solution.py:218
  32.2 14.5 %collective-permute-start.5 = (bf16[128,128]{1,0:T(8,128)(2,1)S(1)}, bf16[128,128]{1,0:T(8,128)(2,1)S(1)}, u32[]{:S(2)}, u32[]{:S(2)}) collective-permute-start(bf16[128,128]{1,0:T(8,128)(2,1)S(1)} %slice.38), channel_id=1, source_target_pairs={{0,56},{1,57},{2,58},{3,59},{4,60},{5,61},{6,62},{7,63},{8,0},{9,1... | collective-permute-start | bytes 98312 | tf_op jit(solution)/shard_map/ppermute | solution.py:218
  46.7 1.8 %collective-permute-done.5 = bf16[128,128]{1,0:T(8,128)(2,1)S(1)} collective-permute-done((bf16[128,128]{1,0:T(8,128)(2,1)S(1)}, bf16[128,128]{1,0:T(8,128)(2,1)S(1)}, u32[]{:S(2)}, u32[]{:S(2)}) %collective-permute-start.5) | collective-permute-done | bytes 32800 | tf_op jit(solution)/shard_map/ppermute | solution.py:218
  48.5 0.2 collective-permute-done.4
  48.7 13.0 %collective-permute-start.6 = (bf16[64,128]{1,0:T(8,128)(2,1)S(1)}, bf16[64,128]{1,0:T(8,128)(2,1)S(1)}, u32[]{:S(2)}, u32[]{:S(2)}) collective-permute-start(bf16[64,128]{1,0:T(8,128)(2,1)S(1)} %fusion), channel_id=1, source_target_pairs={{0,24},{1,25},{2,26},{3,27},{4,28},{5,29},{6,30},{7,31},{8,32},{9,... | collective-permute-start | bytes 49160 | tf_op jit(solution)/shard_map/ppermute | solution.py:218
  61.7 2.7 %collective-permute-start.7 = (bf16[64,128]{1,0:T(8,128)(2,1)S(1)}, bf16[64,128]{1,0:T(8,128)(2,1)S(1)}, u32[]{:S(2)}, u32[]{:S(2)}) collective-permute-start(bf16[64,128]{1,0:T(8,128)(2,1)S(1)} %slice.57), channel_id=1, source_target_pairs={{0,40},{1,41},{2,42},{3,43},{4,44},{5,45},{6,46},{7,47},{8,48},{9,... | collective-permute-start | bytes 49160 | tf_op jit(solution)/shard_map/ppermute | solution.py:218
  64.3 1.7 %collective-permute-done.6 = bf16[64,128]{1,0:T(8,128)(2,1)S(1)} collective-permute-done((bf16[64,128]{1,0:T(8,128)(2,1)S(1)}, bf16[64,128]{1,0:T(8,128)(2,1)S(1)}, u32[]{:S(2)}, u32[]{:S(2)}) %collective-permute-start.6) | collective-permute-done | bytes 16416 | tf_op jit(solution)/shard_map/ppermute | solution.py:218
  66.0 13.0 %collective-permute-done.7 = bf16[64,128]{1,0:T(8,128)(2,1)S(1)} collective-permute-done((bf16[64,128]{1,0:T(8,128)(2,1)S(1)}, bf16[64,128]{1,0:T(8,128)(2,1)S(1)}, u32[]{:S(2)}, u32[]{:S(2)}) %collective-permute-start.7) | collective-permute-done | bytes 16416 | tf_op jit(solution)/shard_map/ppermute | solution.py:218
  79.1 0.7 reshape.11
  (8 shorter events, 0.1 us)
Async XLA Ops:
  0.0 2.8 %collective-permute-start = (bf16[128,1024]{1,0:T(8,128)(2,1)}, bf16[128,1024]{1,0:T(8,128)(2,1)S(1)}, u32[]{:S(2)}, u32[]{:S(2)}) collective-permute-start(bf16[128,1024]{1,0:T(8,128)(2,1)} %bitcast.8), channel_id=1, source_target_pairs={{0,1},{1,0},{2,3},{3,2},{4,5},{5,4},{6,7},{7,6},{8,9},{9,8},{10,11... | collective-permute-start | bytes 786440 | tf_op jit(solution)/shard_map/ppermute | solution.py:155
  0.0 9.3 %collective-permute-start.1 = (bf16[128,1024]{1,0:T(8,128)(2,1)}, bf16[128,1024]{1,0:T(8,128)(2,1)S(1)}, u32[]{:S(2)}, u32[]{:S(2)}) collective-permute-start(bf16[128,1024]{1,0:T(8,128)(2,1)} %bitcast.9), channel_id=1, source_target_pairs={{0,2},{1,3},{2,0},{3,1},{4,6},{5,7},{6,4},{7,5},{8,10},{9,11},{10,... | collective-permute-start | bytes 786440 | tf_op jit(solution)/shard_map/ppermute | solution.py:155
  9.3 1.9 %collective-permute-start.2 = (bf16[128,1024]{1,0:T(8,128)(2,1)S(1)}, bf16[128,1024]{1,0:T(8,128)(2,1)S(1)}, u32[]{:S(2)}, u32[]{:S(2)}) collective-permute-start(bf16[128,1024]{1,0:T(8,128)(2,1)S(1)} %collective-permute-done.1.across.xs), channel_id=1, source_target_pairs={{0,1},{1,0},{2,3},{3,2},{4,5},{5,4},{6,7},{7,6},{8,9},{9,8},{10,11... | collective-permute-start | bytes 786440 | tf_op jit(solution)/shard_map/ppermute | solution.py:155
  11.2 5.9 %copy-start = (bf16[1,1024,2,64]{1,3,2,0:T(8,128)(2,1)S(1)}, bf16[1,1024,2,64]{1,3,2,0:T(8,128)(2,1)}, u32[]{:S(2)}) copy-start(bf16[1,1024,2,64]{1,3,2,0:T(8,128)(2,1)} %param.6) | copy-start | bytes 786436
  13.1 11.0 %collective-permute-start.3 = (bf16[512,128]{1,0:T(8,128)(2,1)S(1)}, bf16[512,128]{1,0:T(8,128)(2,1)S(1)}, u32[]{:S(2)}, u32[]{:S(2)}) collective-permute-start(bf16[512,128]{1,0:T(8,128)(2,1)S(1)} %shard_map.67), channel_id=1, source_target_pairs={{0,4},{1,5},{2,6},{3,7},{4,0},{5,1},{6,2},{7,3},{8,12},{9,13},{10,... | collective-permute-start | bytes 393224 | tf_op jit(solution)/shard_map/ppermute | solution.py:155
  24.1 24.5 %collective-permute-start.4 = (bf16[192,128]{1,0:T(8,128)(2,1)S(1)}, bf16[192,128]{1,0:T(8,128)(2,1)S(1)}, u32[]{:S(2)}, u32[]{:S(2)}) collective-permute-start(bf16[192,128]{1,0:T(8,128)(2,1)S(1)} %slice.36), channel_id=1, source_target_pairs={{0,8},{1,9},{2,10},{3,11},{4,12},{5,13},{6,14},{7,15},{8,16},{9,17... | collective-permute-start | bytes 147464 | tf_op jit(solution)/shard_map/ppermute | solution.py:218
  32.2 16.3 %collective-permute-start.5 = (bf16[128,128]{1,0:T(8,128)(2,1)S(1)}, bf16[128,128]{1,0:T(8,128)(2,1)S(1)}, u32[]{:S(2)}, u32[]{:S(2)}) collective-permute-start(bf16[128,128]{1,0:T(8,128)(2,1)S(1)} %slice.38), channel_id=1, source_target_pairs={{0,56},{1,57},{2,58},{3,59},{4,60},{5,61},{6,62},{7,63},{8,0},{9,1... | collective-permute-start | bytes 98312 | tf_op jit(solution)/shard_map/ppermute | solution.py:218
  48.7 17.4 %collective-permute-start.6 = (bf16[64,128]{1,0:T(8,128)(2,1)S(1)}, bf16[64,128]{1,0:T(8,128)(2,1)S(1)}, u32[]{:S(2)}, u32[]{:S(2)}) collective-permute-start(bf16[64,128]{1,0:T(8,128)(2,1)S(1)} %fusion), channel_id=1, source_target_pairs={{0,24},{1,25},{2,26},{3,27},{4,28},{5,29},{6,30},{7,31},{8,32},{9,... | collective-permute-start | bytes 49160 | tf_op jit(solution)/shard_map/ppermute | solution.py:218
  61.7 17.4 %collective-permute-start.7 = (bf16[64,128]{1,0:T(8,128)(2,1)S(1)}, bf16[64,128]{1,0:T(8,128)(2,1)S(1)}, u32[]{:S(2)}, u32[]{:S(2)}) collective-permute-start(bf16[64,128]{1,0:T(8,128)(2,1)S(1)} %slice.57), channel_id=1, source_target_pairs={{0,40},{1,41},{2,42},{3,43},{4,44},{5,45},{6,46},{7,47},{8,48},{9,... | collective-permute-start | bytes 49160 | tf_op jit(solution)/shard_map/ppermute | solution.py:218
